TPU v7x, 32 devices: a whole 2x2x4 slice. The times are simulated.
32 devices in a mesh: nest: 2 (over core), row: 4 (over y, x), col: 4 (over z).
Axes of the slice: x: 2, y: 2, z: 4, core: 2. Of those that a mesh axis runs over, the one named last changes fastest.
Arguments:
- strips: float32 [2, 3, 4, 16, 24, 1536], P('nest', None, None, ('row', 'col')), may hold values from -1.5 to 2, as said below
- anchor: int32 [2, 2], replicated, may hold values from 1 to 127
- wet_mask: int32 [2, 512, 512], P('nest', 'row', 'col'), may hold values 0 or 1
- bathy_index: int32 [2, 512, 512], P('nest', 'row', 'col'), may hold values from 0 to 15
- bed_levels: float32 [16], replicated, may hold values from 0 to 1.5
- coarse: float32 [3, 1024, 512], P(None, ('nest', 'row'), 'col'), may hold values from -6 to 6
Outputs:
- fine_fields: float32 [2, 3, 1536, 1536], P('nest', None, 'row', 'col')
- coarse_next: float32 [3, 1024, 512], P(None, ('nest', 'row'), 'col')
Inputs may be any that keep to these rules, and one draw needn't show every extreme that they name: `strips`: plane 0 of the second dimension is the water depth, within 0.5 to 2; planes 1 and 2 are momenta within -1.5 to 1.5. anchor[n] holds the row and then the column offset of nest n's first coarse cell within its block of coarse rows.
All inputs are finite; a program needn't handle non-finite values. No bound on the sum of `wet_mask` on one device may be relied on, other than what follows from the above.
Results may differ from a plain program's by a relative error of at most 0.0003.
Values sent between devices are 32-bit elements; how exact they have to be, the bound alone decides.
A program may use at most 128 MiB of HBM per device.

v0:
```python
import functools

import jax
import jax.numpy as jnp
from jax import lax
from jax.experimental import pallas as pl
from jax.experimental.pallas import tpu as pltpu
from jax.sharding import PartitionSpec as P

gravity = 1.0
courant = 0.2
MESH = pl.DeviceIdType.MESH
LANES = 128
SUB = 8
HEAD = 7
VMEM_BYTES = 67043328


def onehot(cond):
    return jnp.where(cond, 1.0, 0.0).astype(jnp.bfloat16)


def iota(shape, dim):
    return lax.broadcasted_iota(jnp.int32, shape, dim)


def dot(a, b):
    return jnp.dot(a, b, preferred_element_type=jnp.float32)


def dot_t(a, b):
    return lax.dot_general(
        a, b, (((1,), (1,)), ((), ())), preferred_element_type=jnp.float32
    )


def split(x, terms):
    parts = []
    for _ in range(terms):
        part = x.astype(jnp.bfloat16)
        parts.append(part)
        x = x - part.astype(jnp.float32)
    return parts


def exchange_kernel(
    rows, cols, strips, wet, cls, fields, colh, rowh, cellh,
    held, wet_v, cls_v, col_msg, row_msg, cell_msg, load_sem,
    big_send, big_recv, col_send, col_recv, row_send, row_recv, cell_send, cell_recv,
):
    parts = rows * cols
    row, col = lax.axis_index("row"), lax.axis_index("col")
    me = row * cols + col
    band = strips.shape[4]
    tile_cols = fields.shape[3]
    full_cols = strips.shape[5]

    loads = [
        pltpu.make_async_copy(strips.at[0, :, :, 0], held, load_sem.at[0]),
        pltpu.make_async_copy(wet.at[0], wet_v, load_sem.at[1]),
        pltpu.make_async_copy(cls.at[0], cls_v, load_sem.at[2]),
    ]
    for load in loads:
        load.start()

    def place(q):
        return {"row": q // cols, "col": lax.rem(q, cols)}

    barrier = pltpu.get_barrier_semaphore()

    def greet(t, _):
        q = lax.rem(me + t, parts)
        pl.semaphore_signal(barrier, inc=1, device_id=place(q), device_id_type=MESH)
        return 0

    lax.fori_loop(1, parts, greet, 0)
    pl.semaphore_wait(barrier, parts - 1)

    def columns(c):
        return pl.ds(pl.multiple_of(c * tile_cols, LANES), tile_cols)

    def big(q):
        return pltpu.make_async_remote_copy(
            src_ref=strips.at[0, :, q // cols, 0, :, columns(lax.rem(q, cols))],
            dst_ref=fields.at[:, me],
            send_sem=big_send.at[q],
            recv_sem=big_recv.at[me],
            device_id=place(q),
            device_id_type=MESH,
        )

    def big_start(t, _):
        big(lax.rem(me + t, parts)).start()
        return 0

    lax.fori_loop(1, parts, big_start, 0)
    own = pltpu.make_async_copy(
        strips.at[0, :, row, 0, :, columns(col)], fields.at[:, me], big_recv.at[me]
    )
    own.start()

    for load in loads:
        load.wait()
    lane = iota((SUB, LANES), 1)
    sub = iota((SUB, LANES), 0)
    first = onehot(lane == 0)
    last = onehot(lane == LANES - 1)
    even = iota((SUB, band), 0)
    for j in range(rows):
        for c in range(cols):
            message = jnp.zeros((SUB, band), jnp.float32)
            for k in range(3):
                if c > 0:
                    for part in split(held[k, j, :, c * tile_cols - LANES : c * tile_cols], 3):
                        message += jnp.where(even == k, dot_t(last, part), 0.0)
                if c < cols - 1:
                    for part in split(
                        held[k, j, :, (c + 1) * tile_cols : (c + 1) * tile_cols + LANES], 3
                    ):
                        message += jnp.where(even == 3 + k, dot_t(first, part), 0.0)
            col_msg[j * cols + c, :, 0:band] = message
    for j in range(rows):
        for k in range(3):
            row_msg[0, j, k : k + 1, :] = held[k, j, band - 1 : band, :]
            row_msg[1, j, k : k + 1, :] = held[k, j, 0:1, :]
    cell_rows = wet_v.shape[0]
    for at, cells in enumerate((wet_v, cls_v)):
        cell_msg[0, at : at + 1, :] = cells[cell_rows - 1 : cell_rows, :]
        cell_msg[1, at : at + 1, :] = cells[0:1, :]
        across = cells[...].astype(jnp.float32).astype(jnp.bfloat16)
        width = across.shape[1]
        pick = iota((SUB, width), 1)
        cell_msg[2, at : at + 1, :] = dot_t(onehot(pick == width - 1), across)[0:1].astype(jnp.int32)
        cell_msg[3, at : at + 1, :] = dot_t(onehot(pick == 0), across)[0:1].astype(jnp.int32)

    def col_copy(q):
        return pltpu.make_async_remote_copy(
            src_ref=col_msg.at[q],
            dst_ref=colh.at[me],
            send_sem=col_send.at[q],
            recv_sem=col_recv.at[me],
            device_id=place(q),
            device_id_type=MESH,
        )

    def col_start(t, _):
        col_copy(lax.rem(me + t, parts)).start()
        return 0

    lax.fori_loop(1, parts, col_start, 0)
    own_col = pltpu.make_async_copy(col_msg.at[me], colh.at[me], col_recv.at[me])
    own_col.start()

    cell_links = (
        (0, row < rows - 1, {"row": row + 1, "col": col}, row > 0),
        (1, row > 0, {"row": row - 1, "col": col}, row < rows - 1),
        (2, col < cols - 1, {"row": row, "col": col + 1}, col > 0),
        (3, col > 0, {"row": row, "col": col - 1}, col < cols - 1),
    )

    def cell_copy(slot, target):
        return pltpu.make_async_remote_copy(
            src_ref=cell_msg.at[slot],
            dst_ref=cellh.at[slot],
            send_sem=cell_send.at[slot],
            recv_sem=cell_recv.at[slot],
            device_id=target,
            device_id_type=MESH,
        )

    for slot, sends, target, _ in cell_links:
        @pl.when(sends)
        def _(slot=slot, target=target):
            cell_copy(slot, target).start()

    def row_copy(slot, j, c):
        target_row = j + 1 if slot == 0 else j - 1
        return pltpu.make_async_remote_copy(
            src_ref=row_msg.at[slot, j, :, c * tile_cols : (c + 1) * tile_cols],
            dst_ref=rowh.at[slot],
            send_sem=row_send.at[slot, j, c],
            recv_sem=row_recv.at[slot],
            device_id={"row": target_row, "col": c},
            device_id_type=MESH,
        )

    def row_own(slot, j, c):
        return pltpu.make_async_copy(
            row_msg.at[slot, j, :, c * tile_cols : (c + 1) * tile_cols],
            rowh.at[slot],
            row_recv.at[slot],
        )

    owner = (rows * cols - 1, 0)
    for slot in range(2):
        @pl.when(me == owner[slot])
        def _(slot=slot):
            for j in range(rows):
                target_row = j + 1 if slot == 0 else j - 1
                if target_row < 0 or target_row >= rows:
                    continue
                for c in range(cols):
                    if target_row * cols + c == owner[slot]:
                        row_own(slot, j, c).start()
                    else:
                        row_copy(slot, j, c).start()

    def arrive(t, _):
        q = lax.rem(me + t, parts)
        pltpu.make_async_copy(fields.at[:, q], fields.at[:, q], big_recv.at[q]).wait()
        pltpu.make_async_copy(colh.at[q], colh.at[q], col_recv.at[q]).wait()
        return 0

    lax.fori_loop(0, parts, arrive, 0)
    for slot, _, target, receives in cell_links:
        @pl.when(receives)
        def _(slot=slot, target=target):
            cell_copy(slot, target).wait_recv()

    for slot, receives in ((0, row > 0), (1, row < rows - 1)):
        @pl.when(receives)
        def _(slot=slot):
            row_own(slot, 0, 0).wait()

    def leave(t, _):
        q = lax.rem(me + t, parts)
        big(q).wait_send()
        col_copy(q).wait_send()
        return 0

    lax.fori_loop(1, parts, leave, 0)
    for slot, sends, target, _ in cell_links:
        @pl.when(sends)
        def _(slot=slot, target=target):
            cell_copy(slot, target).wait_send()
    for slot in range(2):
        @pl.when(me == owner[slot])
        def _(slot=slot):
            for j in range(rows):
                target_row = j + 1 if slot == 0 else j - 1
                if target_row < 0 or target_row >= rows:
                    continue
                for c in range(cols):
                    if target_row * cols + c != owner[slot]:
                        row_copy(slot, j, c).wait_send()


def exchange(rows, cols, strips, wet, cls):
    parts = rows * cols
    blocks, band, full_cols = strips.shape[2], strips.shape[4], strips.shape[5]
    tile_cols = full_cols // cols
    any_spec = pl.BlockSpec(memory_space=pl.ANY)
    dma = pltpu.SemaphoreType.DMA
    f32 = jnp.float32
    return pl.pallas_call(
        functools.partial(exchange_kernel, rows, cols),
        out_shape=(
            jax.ShapeDtypeStruct((3, parts, band, tile_cols), f32),
            jax.ShapeDtypeStruct((parts, SUB, LANES), f32),
            jax.ShapeDtypeStruct((2, SUB, tile_cols), f32),
            jax.ShapeDtypeStruct((4, SUB, LANES), jnp.int32),
        ),
        in_specs=[any_spec] * 3,
        out_specs=(any_spec,) * 4,
        scratch_shapes=[
            pltpu.VMEM((3, blocks, band, full_cols), f32),
            pltpu.VMEM(wet.shape[1:], jnp.int32),
            pltpu.VMEM(cls.shape[1:], jnp.int32),
            pltpu.VMEM((parts, SUB, LANES), f32),
            pltpu.VMEM((2, blocks, SUB, full_cols), f32),
            pltpu.VMEM((4, SUB, LANES), jnp.int32),
            dma((3,)),
            dma((parts,)), dma((parts,)), dma((parts,)), dma((parts,)),
            dma((2, rows, cols)), dma((2,)), dma((4,)), dma((4,)),
        ],
        compiler_params=pltpu.CompilerParams(collective_id=0, has_side_effects=True),
        name="exchange",
    )(strips, wet, cls)


def step_kernel(
    rows, cols, chunk, anchor, levels, fields, edge_cols, rowh, wet, cls, cellh,
    fine, quads, pad, bed_v, wet_p, bed_p,
):
    nest, row, col = lax.axis_index("nest"), lax.axis_index("row"), lax.axis_index("col")
    tile_rows, tile_cols = fields.shape[1], fields.shape[2]
    cell_rows, cell_cols = wet.shape
    wide = tile_cols + LANES
    above, below = row > 0, row < rows - 1
    left, right = col > 0, col < cols - 1
    end = SUB + tile_rows

    def look(classes):
        bed = jnp.zeros(classes.shape, jnp.float32)
        for at in range(levels.shape[0]):
            bed = jnp.where(classes == at, levels[at], bed)
        return bed

    down = onehot(iota((tile_rows, cell_rows), 0) // 3 == iota((tile_rows, cell_rows), 1))
    across = onehot(iota((cell_cols, tile_cols), 1) // 3 == iota((cell_cols, tile_cols), 0))
    lane = iota((tile_rows, LANES), 1)

    def side(low, high):
        low = jnp.where(left, low, 0.0)
        high = jnp.where(right, high, 0.0)
        return jnp.where(lane == 0, high, jnp.where(lane == LANES - 1, low, 0.0))

    edge = cellh[...]
    edge_bed = [look(edge[slot]) for slot in range(4)]
    edge_wet = [edge[slot].astype(jnp.float32) for slot in range(4)]
    bed_v[...] = look(cls[...])
    for target, inner, edges, at, terms in (
        (wet_p, wet[...].astype(jnp.float32), edge_wet, 0, 1),
        (bed_p, bed_v[...], edge_bed, 1, 3),
    ):
        full = 0.0
        for part in split(inner, terms):
            full += dot(dot(down, part).astype(jnp.bfloat16), across)
        target[SUB:end, 0:tile_cols] = full

        def row_of(slot):
            total = 0.0
            for part in split(edges[slot], terms):
                total += dot(part, across)
            return total[at : at + 1]

        def col_of(slot):
            total = 0.0
            for part in split(edges[slot], terms):
                total += dot_t(down, part)
            return total[:, at : at + 1]

        zeros = jnp.zeros((SUB, wide), jnp.float32)
        target[0:SUB, :] = zeros
        target[end : end + SUB, :] = zeros
        target[SUB - 1 : SUB, 0:tile_cols] = jnp.where(above, row_of(0), 0.0)
        target[end : end + 1, 0:tile_cols] = jnp.where(below, row_of(1), 0.0)
        target[SUB:end, tile_cols:wide] = side(col_of(2), col_of(3))

    for k in range(3):
        pad[k, SUB:end, 0:tile_cols] = fields[k]
        pad[k, 0:SUB, :] = jnp.zeros((SUB, wide), jnp.float32)
        pad[k, end : end + SUB, :] = jnp.zeros((SUB, wide), jnp.float32)
        pad[k, SUB - 1 : SUB, 0:tile_cols] = jnp.where(above, rowh[0, k : k + 1, :], 0.0)
        pad[k, end : end + 1, 0:tile_cols] = jnp.where(below, rowh[1, k : k + 1, :], 0.0)
        pad[k, SUB:end, tile_cols:wide] = side(
            edge_cols[:, k : k + 1], edge_cols[:, 3 + k : 4 + k]
        )

    window = chunk + 2 * SUB

    def west(x):
        return pltpu.roll(x, 1, 1)

    def east(x):
        return pltpu.roll(x, wide - 1, 1)

    def north(x):
        return pltpu.roll(x, 1, 0)

    def south(x):
        return pltpu.roll(x, x.shape[0] - 1, 0)

    def body(step, _):
        base = pl.multiple_of(step * chunk, SUB)
        at = pl.ds(base, window)
        h, hu, hv = pad[0, at, :], pad[1, at, :], pad[2, at, :]
        wet_w, bed_w = wet_p[at, :], bed_p[at, :]
        safe = jnp.where(wet_w > 0.5, h, 1.0)
        inverse = 1.0 / safe
        u, v = hu * inverse, hv * inverse
        speed = safe * lax.rsqrt(safe)
        pressure = 0.5 * gravity * safe * safe
        cross = hu * v

        def mid(x):
            return x[SUB : SUB + chunk]

        def narrow(x):
            return x[:, 0:tile_cols]

        h_n, hu_n, hv_n, wet_n, bed_n = [narrow(x) for x in (h, hu, hv, wet_w, bed_w)]
        gate = (0.5 * courant) * (north(wet_n) * wet_n)
        reach = narrow(jnp.abs(v) + speed)
        bound = jnp.maximum(north(reach), reach)
        totals = []
        for state, flux in (
            (h_n, hv_n), (hu_n, narrow(cross)), (hv_n, narrow(hv * v + pressure)),
        ):
            face = gate * ((north(flux) + flux) - bound * (state - north(state)))
            totals.append(mid(face) - mid(south(face)))
        slope = gate * (bed_n - north(bed_n))
        centre = mid(h_n)
        totals[2] -= gravity * centre * (mid(slope) + mid(south(slope)))

        h_m, hu_m, hv_m, wet_m, bed_m = [mid(x) for x in (h, hu, hv, wet_w, bed_w)]
        gate = (0.5 * courant) * (west(wet_m) * wet_m)
        reach = mid(jnp.abs(u) + speed)
        bound = jnp.maximum(west(reach), reach)
        for k, (state, flux) in enumerate(
            ((h_m, hu_m), (hu_m, mid(hu * u + pressure)), (hv_m, mid(cross)))
        ):
            face = gate * ((west(flux) + flux) - bound * (state - west(state)))
            totals[k] += narrow(face - east(face))
        slope = gate * (bed_m - west(bed_m))
        totals[1] -= gravity * centre * narrow(slope + east(slope))
        out = pl.ds(base, chunk)
        for k, state in enumerate((h_m, hu_m, hv_m)):
            fine[0, k, out, :] = narrow(state) + totals[k]
        return 0

    lax.fori_loop(0, tile_rows // chunk, body, 0)

    shift_r, shift_c = anchor[nest, 0], anchor[nest, 1]
    low = onehot(
        iota((2 * cell_rows, tile_rows), 1) // 3 + shift_r == iota((2 * cell_rows, tile_rows), 0)
    )
    wide_pick = onehot(
        iota((tile_cols, 2 * cell_cols), 0) // 3 + shift_c == iota((tile_cols, 2 * cell_cols), 1)
    )
    for k in range(3):
        part_rows = 0.0
        for part in split(fine[0, k], 2):
            part_rows += dot(low, part)
        placed = 0.0
        for part in split(part_rows, 2):
            placed += dot(part, wide_pick)
        placed = placed * (1.0 / 9.0)
        for a in range(2):
            for b in range(2):
                quads[2 * a + b, k] = placed[
                    a * cell_rows : (a + 1) * cell_rows, b * cell_cols : (b + 1) * cell_cols
                ]


def step(rows, cols, anchor, levels, fields, edge_cols, rowh, wet, cls, cellh):
    tile_rows, tile_cols = fields.shape[1:]
    cell_rows, cell_cols = wet.shape
    smem = pl.BlockSpec(memory_space=pltpu.SMEM)
    vmem = pl.BlockSpec(memory_space=pltpu.VMEM)
    f32 = jnp.float32
    padded = (tile_rows + 2 * SUB, tile_cols + LANES)
    return pl.pallas_call(
        functools.partial(step_kernel, rows, cols, 48),
        out_shape=(
            jax.ShapeDtypeStruct((1, 3, tile_rows, tile_cols), f32),
            jax.ShapeDtypeStruct((4, 3, cell_rows, cell_cols), f32),
        ),
        in_specs=[smem, smem] + [vmem] * 6,
        out_specs=(vmem, vmem),
        scratch_shapes=[
            pltpu.VMEM((3,) + padded, f32),
            pltpu.VMEM(wet.shape, f32),
            pltpu.VMEM(padded, f32),
            pltpu.VMEM(padded, f32),
        ],
        compiler_params=pltpu.CompilerParams(vmem_limit_bytes=40 * 1024 * 1024),
        name="step",
    )(anchor, levels, fields, edge_cols, rowh, wet, cls, cellh)


def feedback_kernel(nests, rows, cols, anchor, quads, coarse, out, held, send_sem, recv_sem):
    nest, row, col = lax.axis_index("nest"), lax.axis_index("row"), lax.axis_index("col")
    block = nest * rows + row
    blocks = nests * rows
    cell_rows, cell_cols = coarse.shape[1], coarse.shape[2]

    def place(b, c):
        return {"nest": b // rows, "row": lax.rem(b, rows), "col": c}

    links = []
    for quad in (1, 2, 3):
        db, dc = quad // 2, quad % 2
        sends = jnp.logical_and(block + db < blocks, col + dc < cols)
        takes = jnp.logical_and(block - db >= 0, col - dc >= 0)
        links.append((quad, sends, place(block + db, col + dc), takes, place(block - db, col - dc)))

    barrier = pltpu.get_barrier_semaphore()
    for _, _, _, takes, source in links:
        @pl.when(takes)
        def _(source=source):
            pl.semaphore_signal(barrier, inc=1, device_id=source, device_id_type=MESH)
    targets = sum(jnp.where(sends, 1, 0) for _, sends, _, _, _ in links)

    @pl.when(targets > 0)
    def _():
        pl.semaphore_wait(barrier, targets)

    def copy(quad, target):
        return pltpu.make_async_remote_copy(
            src_ref=quads.at[quad],
            dst_ref=held.at[quad - 1],
            send_sem=send_sem.at[quad - 1],
            recv_sem=recv_sem.at[quad - 1],
            device_id=target,
            device_id_type=MESH,
        )

    for quad, sends, target, _, _ in links:
        @pl.when(sends)
        def _(quad=quad, target=target):
            copy(quad, target).start()

    at_row = block * cell_rows + iota((cell_rows, cell_cols), 0)
    at_col = col * cell_cols + iota((cell_rows, cell_cols), 1)
    count = jnp.ones((cell_rows, cell_cols), jnp.float32)
    for n in range(nests):
        from_row = at_row - (n * rows * cell_rows + anchor[n, 0])
        from_col = at_col - anchor[n, 1]
        inside = (from_row >= 0) & (from_row < rows * cell_rows)
        inside &= (from_col >= 0) & (from_col < cols * cell_cols)
        count += jnp.where(inside, 1.0, 0.0)
    weight = 1.0 / count
    for k in range(3):
        out[k] = coarse[k] + quads[0, k]
    for quad, _, target, takes, _ in links:
        @pl.when(takes)
        def _(quad=quad, target=target):
            copy(quad, target).wait_recv()
            for k in range(3):
                out[k] += held[quad - 1, k]
    for k in range(3):
        out[k] = out[k] * weight
    for quad, sends, target, _, _ in links:
        @pl.when(sends)
        def _(quad=quad, target=target):
            copy(quad, target).wait_send()


def feedback(nests, rows, cols, anchor, quads, coarse):
    smem = pl.BlockSpec(memory_space=pltpu.SMEM)
    vmem = pl.BlockSpec(memory_space=pltpu.VMEM)
    return pl.pallas_call(
        functools.partial(feedback_kernel, nests, rows, cols),
        out_shape=jax.ShapeDtypeStruct(coarse.shape, jnp.float32),
        in_specs=[smem, vmem, vmem],
        out_specs=vmem,
        scratch_shapes=[
            pltpu.VMEM((3,) + coarse.shape, jnp.float32),
            pltpu.SemaphoreType.DMA((3,)),
            pltpu.SemaphoreType.DMA((3,)),
        ],
        compiler_params=pltpu.CompilerParams(collective_id=1, has_side_effects=True),
        name="feedback",
    )(anchor, quads, coarse)


def fused_kernel(
    nests, rows, cols, anchor_in, levels_in, strips, wet, cls, coarse, fine, out,
    anchor, levels, fine_sem, held, wet_v, cls_v, coarse_v, pad, wet_p, bed_p, colh, rowh, cellh,
    col_msg, row_msg, cell_msg, rest, above, spill, taken, load_sem,
    big_send, big_recv, col_send, col_recv, row_send, row_recv, cell_send, cell_recv,
    down_send, down_recv, side_send, side_recv,
):
    parts = rows * cols
    nest, row, col = lax.axis_index("nest"), lax.axis_index("row"), lax.axis_index("col")
    me = row * cols + col
    block, blocks = nest * rows + row, nests * rows
    band = strips.shape[4]
    tile_rows, tile_cols = fine.shape[2], fine.shape[3]
    cell_rows, cell_cols = wet_v.shape
    group = band // 3
    wide = tile_cols + LANES
    end = SUB + tile_rows
    has_above, has_below = row > 0, row < rows - 1
    has_left, has_right = col > 0, col < cols - 1

    loads = [
        pltpu.make_async_copy(strips.at[0, :, :, 0], held, load_sem.at[0]),
        pltpu.make_async_copy(wet.at[0], wet_v, load_sem.at[1]),
        pltpu.make_async_copy(cls.at[0], cls_v, load_sem.at[2]),
        pltpu.make_async_copy(coarse, coarse_v, load_sem.at[3]),
        pltpu.make_async_copy(anchor_in, anchor, load_sem.at[4]),
        pltpu.make_async_copy(levels_in, levels, load_sem.at[5]),
    ]
    for load in loads:
        load.start()

    def place(q):
        return {"row": q // cols, "col": lax.rem(q, cols)}

    barrier = pltpu.get_barrier_semaphore()
    to_next = jnp.logical_and(row == rows - 1, nest < nests - 1)
    to_last = jnp.logical_and(row == 0, nest > 0)
    below_id = {"nest": (block + 1) // rows, "row": lax.rem(block + 1, rows), "col": col}

    def greet(t, _):
        q = lax.rem(me + t, parts)
        pl.semaphore_signal(barrier, inc=1, device_id=place(q), device_id_type=MESH)
        return 0

    lax.fori_loop(1, parts, greet, 0)

    @pl.when(to_next)
    def _():
        pl.semaphore_signal(barrier, inc=1, device_id=below_id, device_id_type=MESH)

    @pl.when(to_last)
    def _():
        pl.semaphore_signal(
            barrier, inc=1, device_id={"nest": nest - 1, "row": rows - 1, "col": col},
            device_id_type=MESH,
        )

    peers = parts - 1 + jnp.where(to_next, 1, 0) + jnp.where(to_last, 1, 0)
    pl.semaphore_wait(barrier, peers)

    def columns(c):
        return pl.ds(pl.multiple_of(c * tile_cols, LANES), tile_cols)

    def landing(p):
        return pad.at[:, pl.ds(pl.multiple_of(SUB + p * band, SUB), band), 0:tile_cols]

    def big(q):
        return pltpu.make_async_remote_copy(
            src_ref=strips.at[0, :, q // cols, 0, :, columns(lax.rem(q, cols))],
            dst_ref=landing(me),
            send_sem=big_send.at[q],
            recv_sem=big_recv.at[me],
            device_id=place(q),
            device_id_type=MESH,
        )

    def big_start(t, _):
        big(lax.rem(me + t, parts)).start()
        return 0

    early = min(parts, HEAD)
    lax.fori_loop(1, early, big_start, 0)
    own = pltpu.make_async_copy(
        strips.at[0, :, row, 0, :, columns(col)], landing(me), big_recv.at[me]
    )
    own.start()

    loads[1].wait()
    loads[2].wait()
    for at, cells in enumerate((wet_v, cls_v)):
        cell_msg[0, at : at + 1, :] = cells[cell_rows - 1 : cell_rows, :]
        cell_msg[1, at : at + 1, :] = cells[0:1, :]
        across = cells[...].astype(jnp.float32).astype(jnp.bfloat16)
        pick = iota((SUB, cell_cols), 1)
        cell_msg[2, at : at + 1, :] = dot_t(onehot(pick == cell_cols - 1), across)[0:1].astype(jnp.int32)
        cell_msg[3, at : at + 1, :] = dot_t(onehot(pick == 0), across)[0:1].astype(jnp.int32)
    loads[0].wait()
    for j in range(rows):
        for k in range(3):
            row_msg[0, j, k : k + 1, :] = held[k, j, band - 1 : band, :]
            row_msg[1, j, k : k + 1, :] = held[k, j, 0:1, :]
    lane = iota((SUB, LANES), 1)
    first = onehot(lane == 0)
    last = onehot(lane == LANES - 1)
    slot_of = iota((SUB, band), 0)
    col_msg[...] = jnp.zeros_like(col_msg)
    for j in range(rows):
        for c in range(cols):
            message = jnp.zeros((SUB, band), jnp.float32)
            for k in range(3):
                if c > 0:
                    for part in split(held[k, j, :, c * tile_cols - LANES : c * tile_cols], 3):
                        message += jnp.where(slot_of == k, dot_t(last, part), 0.0)
                if c < cols - 1:
                    for part in split(
                        held[k, j, :, (c + 1) * tile_cols : (c + 1) * tile_cols + LANES], 3
                    ):
                        message += jnp.where(slot_of == 3 + k, dot_t(first, part), 0.0)
            col_msg[j * cols + c, :, 0:band] = message

    cell_links = (
        (0, has_below, {"row": row + 1, "col": col}, has_above),
        (1, has_above, {"row": row - 1, "col": col}, has_below),
        (2, has_right, {"row": row, "col": col + 1}, has_left),
        (3, has_left, {"row": row, "col": col - 1}, has_right),
    )

    def cell_copy(slot, target):
        return pltpu.make_async_remote_copy(
            src_ref=cell_msg.at[slot],
            dst_ref=cellh.at[slot],
            send_sem=cell_send.at[slot],
            recv_sem=cell_recv.at[slot],
            device_id=target,
            device_id_type=MESH,
        )

    for slot, sends, target, _ in cell_links:
        @pl.when(sends)
        def _(slot=slot, target=target):
            cell_copy(slot, target).start()

    def row_copy(slot, j, c):
        return pltpu.make_async_remote_copy(
            src_ref=row_msg.at[slot, j, :, c * tile_cols : (c + 1) * tile_cols],
            dst_ref=rowh.at[slot],
            send_sem=row_send.at[slot, j, c],
            recv_sem=row_recv.at[slot],
            device_id={"row": j + 1 if slot == 0 else j - 1, "col": c},
            device_id_type=MESH,
        )

    def row_own(slot, j, c):
        return pltpu.make_async_copy(
            row_msg.at[slot, j, :, c * tile_cols : (c + 1) * tile_cols],
            rowh.at[slot],
            row_recv.at[slot],
        )

    owner = (parts - 1, 0)

    def row_targets(slot):
        for j in range(rows):
            target_row = j + 1 if slot == 0 else j - 1
            if 0 <= target_row < rows:
                for c in range(cols):
                    yield j, c, target_row * cols + c == owner[slot]

    for slot in range(2):
        @pl.when(me == owner[slot])
        def _(slot=slot):
            for j, c, mine in row_targets(slot):
                (row_own if mine else row_copy)(slot, j, c).start()

    def col_copy(q):
        return pltpu.make_async_remote_copy(
            src_ref=col_msg.at[q],
            dst_ref=colh.at[me],
            send_sem=col_send.at[q],
            recv_sem=col_recv.at[me],
            device_id=place(q),
            device_id_type=MESH,
        )

    def col_start(t, _):
        col_copy(lax.rem(me + t, parts)).start()
        return 0

    lax.fori_loop(1, parts, col_start, 0)
    pltpu.make_async_copy(col_msg.at[me], colh.at[me], col_recv.at[me]).start()
    if early < parts:
        lax.fori_loop(early, parts, big_start, 0)

    loads[4].wait()
    loads[5].wait()

    def look(classes):
        bed = jnp.zeros(classes.shape, jnp.float32)
        for at in range(levels.shape[0]):
            bed = jnp.where(classes == at, levels[at], bed)
        return bed

    down = onehot(iota((tile_rows, cell_rows), 0) // 3 == iota((tile_rows, cell_rows), 1))
    across = onehot(iota((cell_cols, tile_cols), 1) // 3 == iota((cell_cols, tile_cols), 0))

    def side(low, high):
        lane = iota((low.shape[0], LANES), 1)
        low = jnp.where(has_left, low, 0.0)
        high = jnp.where(has_right, high, 0.0)
        return jnp.where(lane == 0, high, jnp.where(lane == LANES - 1, low, 0.0))

    inner = (wet_v[...].astype(jnp.float32), look(cls_v[...]))
    zeros = jnp.zeros((SUB, wide), jnp.float32)
    for target, cells, terms in ((wet_p, inner[0], 1), (bed_p, inner[1], 3)):
        full = 0.0
        for part in split(cells, terms):
            full += dot(dot(down, part).astype(jnp.bfloat16), across)
        target[SUB:end, 0:tile_cols] = full
        target[0:SUB, :] = zeros
        target[end : end + SUB, :] = zeros
    for k in range(3):
        pad[k, 0:SUB, :] = zeros
        pad[k, end : end + SUB, :] = zeros
        pad[k, SUB:end, tile_cols:wide] = jnp.zeros((tile_rows, LANES), jnp.float32)

    for slot, _, target, receives in cell_links:
        @pl.when(jnp.logical_not(receives))
        def _(slot=slot):
            cellh[slot] = jnp.zeros((SUB, LANES), jnp.int32)

        @pl.when(receives)
        def _(slot=slot, target=target):
            cell_copy(slot, target).wait_recv()

    sub = iota((SUB, LANES), 0)
    for target, at, terms in ((wet_p, 0, 1), (bed_p, 1, 3)):
        def edge_of(slot, at=at):
            cells = jnp.where(sub < 2, cellh[slot], 0)
            return cells.astype(jnp.float32) if at == 0 else look(cells)

        def row_of(slot, at=at, terms=terms):
            total = 0.0
            for part in split(edge_of(slot), terms):
                total += dot(part, across)
            return total[at : at + 1]

        def col_of(slot, at=at, terms=terms):
            total = 0.0
            for part in split(edge_of(slot), terms):
                total += dot_t(down, part)
            return total[:, at : at + 1]

        target[SUB - 1 : SUB, 0:tile_cols] = jnp.where(has_above, row_of(0), 0.0)
        target[end : end + 1, 0:tile_cols] = jnp.where(has_below, row_of(1), 0.0)
        target[SUB:end, tile_cols:wide] = side(col_of(2), col_of(3))

    for slot, receives, at in ((0, has_above, SUB - 1), (1, has_below, end)):
        @pl.when(receives)
        def _(slot=slot, at=at):
            row_own(slot, 0, 0).wait()
            for k in range(3):
                pad[k, at : at + 1, 0:tile_cols] = rowh[slot, k : k + 1, :]

    third = onehot(iota((group, band), 1) // 3 == iota((group, band), 0))
    pick = onehot(iota((tile_cols, cell_cols), 0) // 3 == iota((tile_cols, cell_cols), 1))
    unit = onehot(iota((band, LANES), 0) == iota((band, LANES), 1))
    window = band + 2 * SUB

    def west(x):
        return pltpu.roll(x, 1, 1)

    def east(x):
        return pltpu.roll(x, wide - 1, 1)

    def north(x):
        return pltpu.roll(x, 1, 0)

    def south(x):
        return pltpu.roll(x, x.shape[0] - 1, 0)

    def mid(x):
        return x[SUB : SUB + band]

    def narrow(x):
        return x[:, 0:tile_cols]

    def big_wait(b):
        pltpu.make_async_copy(landing(b), landing(b), big_recv.at[b]).wait()

    def rest_rows(ref, b):
        return ref.at[:, pl.ds(pl.multiple_of(b * group, SUB), group), :]

    def down_copy(b):
        return pltpu.make_async_remote_copy(
            src_ref=rest_rows(rest, b),
            dst_ref=rest_rows(above, b),
            send_sem=down_send.at[b],
            recv_sem=down_recv.at[b],
            device_id=below_id,
            device_id_type=MESH,
        )

    def band_at(s):
        return lax.rem(me - 1 - s + 2 * parts, parts)

    def body(s, _):
        b = band_at(s)

        @pl.when(s == 0)
        def _():
            big_wait(me)
            big_wait(band_at(0))

        @pl.when(s < parts - 2)
        def _():
            big_wait(band_at(s + 1))

        pltpu.make_async_copy(colh.at[b], colh.at[b], col_recv.at[b]).wait()
        base = pl.multiple_of(b * band, SUB)
        inside = pl.ds(pl.multiple_of(base + SUB, SUB), band)
        edges = 0.0
        for part in split(colh[b], 3):
            edges += dot_t(unit, part)
        for k in range(3):
            pad[k, inside, tile_cols:wide] = side(edges[:, k : k + 1], edges[:, 3 + k : 4 + k])

        at = pl.ds(base, window)
        h, hu, hv = pad[0, at, :], pad[1, at, :], pad[2, at, :]
        wet_w, bed_w = wet_p[at, :], bed_p[at, :]
        safe = jnp.where(wet_w > 0.5, h, 1.0)
        inverse = 1.0 / safe
        u, v = hu * inverse, hv * inverse
        speed = safe * lax.rsqrt(safe)
        pressure = 0.5 * gravity * safe * safe
        cross = hu * v

        h_n, hu_n, hv_n, wet_n, bed_n = [narrow(x) for x in (h, hu, hv, wet_w, bed_w)]
        gate = (0.5 * courant) * (north(wet_n) * wet_n)
        reach = narrow(jnp.abs(v) + speed)
        bound = jnp.maximum(north(reach), reach)
        totals = []
        for state, flux in (
            (h_n, hv_n), (hu_n, narrow(cross)), (hv_n, narrow(hv * v + pressure)),
        ):
            face = gate * ((north(flux) + flux) - bound * (state - north(state)))
            totals.append(mid(face) - mid(south(face)))
        slope = gate * (bed_n - north(bed_n))
        centre = mid(h_n)
        totals[2] -= gravity * centre * (mid(slope) + mid(south(slope)))

        h_m, hu_m, hv_m, wet_m, bed_m = [mid(x) for x in (h, hu, hv, wet_w, bed_w)]
        gate = (0.5 * courant) * (west(wet_m) * wet_m)
        reach = mid(jnp.abs(u) + speed)
        bound = jnp.maximum(west(reach), reach)
        for k, (state, flux) in enumerate(
            ((h_m, hu_m), (hu_m, mid(hu * u + pressure)), (hv_m, mid(cross)))
        ):
            face = gate * ((west(flux) + flux) - bound * (state - west(state)))
            totals[k] += narrow(face - east(face))
        slope = gate * (bed_m - west(bed_m))
        totals[1] -= gravity * centre * narrow(slope + east(slope))
        cells = pl.ds(pl.multiple_of(b * group, SUB), group)
        for k, state in enumerate((h_m, hu_m, hv_m)):
            value = narrow(state) + totals[k]
            fine[0, k, pl.ds(base, band), :] = value
            summed = 0.0
            for part in split(value, 2):
                summed += dot(third, part)
            mean = 0.0
            for part in split(summed, 2):
                mean += dot(part, pick)
            rest[k, cells, :] = mean * (1.0 / 9.0)

        @pl.when(jnp.logical_and(s > 0, block < blocks - 1))
        def _():
            down_copy(band_at(s - 1)).start()

        return 0

    lax.fori_loop(0, parts, body, 0)

    at_row = block * cell_rows + iota((cell_rows, cell_cols), 0)
    at_col = col * cell_cols + iota((cell_rows, cell_cols), 1)
    count = jnp.ones((cell_rows, cell_cols), jnp.float32)
    for n in range(nests):
        from_row = at_row - (n * rows * cell_rows + anchor[n, 0])
        from_col = at_col - anchor[n, 1]
        covered = (from_row >= 0) & (from_row < rows * cell_rows)
        covered &= (from_col >= 0) & (from_col < cols * cell_cols)
        count += jnp.where(covered, 1.0, 0.0)
    weight = 1.0 / count

    @pl.when(block < blocks - 1)
    def _():
        down_copy(me).start()

    @pl.when(block == 0)
    def _():
        above[...] = jnp.zeros_like(above)

    def down_wait(b, _):
        down_copy(b).wait_recv()
        return 0

    @pl.when(block > 0)
    def _():
        lax.fori_loop(0, parts, down_wait, 0)

    source = jnp.maximum(block - 1, 0) // rows
    r_at, r_from = iota((cell_rows, cell_rows), 0), iota((cell_rows, cell_rows), 1)
    low_own = onehot(r_from + anchor[nest, 0] == r_at)
    low_above = onehot(r_from + anchor[source, 0] == r_at + cell_rows)
    c_from, c_at = iota((cell_cols, 2 * cell_cols), 0), iota((cell_cols, 2 * cell_cols), 1)
    over_own = onehot(c_from + anchor[nest, 1] == c_at)
    over_above = onehot(c_from + anchor[source, 1] == c_at)

    def side_copy(k):
        return pltpu.make_async_remote_copy(
            src_ref=spill.at[k],
            dst_ref=taken.at[k],
            send_sem=side_send.at[k],
            recv_sem=side_recv.at[k],
            device_id={"col": col + 1},
            device_id_type=MESH,
        )

    def side_start(k):
        @pl.when(has_right)
        def _():
            side_copy(k).start()

    loads[3].wait()
    for k in range(3):
        placed = 0.0
        for cells, low, over in ((rest, low_own, over_own), (above, low_above, over_above)):
            moved = 0.0
            for part in split(cells[k], 2):
                moved += dot(low, part)
            for part in split(moved, 2):
                placed += dot(part, over)
        spill[k] = placed[:, cell_cols:]
        if k > 0:
            side_start(k - 1)
        out[k] = coarse_v[k] + placed[:, :cell_cols]
    side_start(2)
    for k in range(3):
        @pl.when(has_left)
        def _(k=k):
            side_copy(k).wait_recv()
            out[k] = (out[k] + taken[k]) * weight

        @pl.when(jnp.logical_not(has_left))
        def _(k=k):
            out[k] = out[k] * weight

    def leave(t, _):
        q = lax.rem(me + t, parts)
        big(q).wait_send()
        col_copy(q).wait_send()
        return 0

    lax.fori_loop(1, parts, leave, 0)

    for slot, sends, target, _ in cell_links:
        @pl.when(sends)
        def _(slot=slot, target=target):
            cell_copy(slot, target).wait_send()
    for slot in range(2):
        @pl.when(me == owner[slot])
        def _(slot=slot):
            for j, c, mine in row_targets(slot):
                if not mine:
                    row_copy(slot, j, c).wait_send()

    def down_leave(b, _):
        down_copy(b).wait_send()
        return 0

    @pl.when(block < blocks - 1)
    def _():
        lax.fori_loop(0, parts, down_leave, 0)

    @pl.when(has_right)
    def _():
        for k in range(3):
            side_copy(k).wait_send()


def fused(nests, rows, cols, strips, anchor, wet, cls, levels, coarse):
    parts = rows * cols
    blocks, band, full_cols = strips.shape[2], strips.shape[4], strips.shape[5]
    tile_rows, tile_cols = parts * band, full_cols // cols
    cells = wet.shape[1:]
    vmem = pl.BlockSpec(memory_space=pltpu.VMEM)
    hbm = pl.BlockSpec(memory_space=pltpu.HBM)
    dma = pltpu.SemaphoreType.DMA
    f32, i32 = jnp.float32, jnp.int32
    padded = (tile_rows + 2 * SUB, tile_cols + LANES)
    results = 4 * (3 * tile_rows * tile_cols + coarse.size)
    return pl.pallas_call(
        functools.partial(fused_kernel, nests, rows, cols),
        out_shape=(
            pltpu.VMEM((1, 3, tile_rows, tile_cols), f32),
            pltpu.VMEM(coarse.shape, f32),
        ),
        in_specs=[hbm] * 6,
        out_specs=(vmem, vmem),
        scratch_shapes=[
            pltpu.SMEM(anchor.shape, i32),
            pltpu.SMEM(levels.shape, f32),
            dma((parts,)),
            pltpu.VMEM((3, blocks, band, full_cols), f32),
            pltpu.VMEM(cells, i32),
            pltpu.VMEM(cells, i32),
            pltpu.VMEM(coarse.shape, f32),
            pltpu.VMEM((3,) + padded, f32),
            pltpu.VMEM(padded, f32),
            pltpu.VMEM(padded, f32),
            pltpu.VMEM((parts, SUB, LANES), f32),
            pltpu.VMEM((2, SUB, tile_cols), f32),
            pltpu.VMEM((4, SUB, LANES), i32),
            pltpu.VMEM((parts, SUB, LANES), f32),
            pltpu.VMEM((2, blocks, SUB, full_cols), f32),
            pltpu.VMEM((4, SUB, LANES), i32),
            pltpu.VMEM(coarse.shape, f32),
            pltpu.VMEM(coarse.shape, f32),
            pltpu.VMEM(coarse.shape, f32),
            pltpu.VMEM(coarse.shape, f32),
            dma((6,)),
            dma((parts,)), dma((parts,)), dma((parts,)), dma((parts,)),
            dma((2, rows, cols)), dma((2,)), dma((4,)), dma((4,)),
            dma((parts,)), dma((parts,)), dma((3,)), dma((3,)),
        ],
        compiler_params=pltpu.CompilerParams(
            collective_id=2, has_side_effects=True, vmem_limit_bytes=VMEM_BYTES - results
        ),
        name="fused",
    )(anchor, levels, strips, wet, cls, coarse)


def emit_kernel(fine, coarse, fine_out, coarse_out, sems):
    copies = [
        pltpu.make_async_copy(fine, fine_out, sems.at[0]),
        pltpu.make_async_copy(coarse, coarse_out, sems.at[1]),
    ]
    for copy in copies:
        copy.start()
    for copy in copies:
        copy.wait()


def emit(fine, coarse):
    vmem = pl.BlockSpec(memory_space=pltpu.VMEM)
    hbm = pl.BlockSpec(memory_space=pl.ANY)
    return pl.pallas_call(
        emit_kernel,
        out_shape=(
            jax.ShapeDtypeStruct(fine.shape, jnp.float32),
            jax.ShapeDtypeStruct(coarse.shape, jnp.float32),
        ),
        in_specs=[vmem, vmem],
        out_specs=(hbm, hbm),
        scratch_shapes=[pltpu.SemaphoreType.DMA((2,))],
        compiler_params=pltpu.CompilerParams(vmem_limit_bytes=4 * 2**20),
        name="emit",
    )(fine, coarse)


def local(nests, rows, cols, strips, anchor, wet_mask, bathy_index, bed_levels, coarse):
    band = strips.shape[4]
    if band % (3 * SUB) == 0:
        return emit(*fused(
            nests, rows, cols, strips, anchor, wet_mask, bathy_index, bed_levels, coarse
        ))
    fields, colh, rowh, cellh = exchange(rows, cols, strips, wet_mask, bathy_index)
    fields = fields.reshape(3, -1, fields.shape[3])
    edge_cols = colh[:, :, :band].transpose(0, 2, 1).reshape(-1, SUB)
    updated, quads = step(
        rows, cols, anchor, bed_levels, fields, edge_cols, rowh, wet_mask[0], bathy_index[0], cellh
    )
    return updated, feedback(nests, rows, cols, anchor, quads, coarse)


def solution(mesh):
    sizes = (mesh.shape["nest"], mesh.shape["row"], mesh.shape["col"])
    return jax.shard_map(
        functools.partial(local, *sizes),
        mesh=mesh,
        in_specs=(
            P("nest", None, None, ("row", "col"), None, None),
            P(),
            P("nest", "row", "col"),
            P("nest", "row", "col"),
            P(),
            P(None, ("nest", "row"), "col"),
        ),
        out_specs=(P("nest", None, "row", "col"), P(None, ("nest", "row"), "col")),
        check_vma=False,
    )
```

profile of v0, /device:TPU:25, one launch (start us, length us, event | category | flops | bytes accessed | tf_op | source)
XLA Modules:
  0.0 62.1 jit_solution(9816389813780640101)
XLA Ops:
  0.6 60.2 %fused.1 = (f32[1,3,384,384]{3,2,1,0:T(8,128)S(1)}, f32[3,128,128]{2,1,0:T(8,128)S(1)}) custom-call(s32[2,2]{1,0:T(2,128)} %anchor_in.1, f32[16]{0:T(128)} %levels_in.1, f32[1,3,4,1,24,1536]{5,4,3,2,1,0:T(8,128)} %strips.1, s32[1,128,128]{2,1,0:T(8,128)} %wet.1, s32[1,128,128]{2,1,0:T(8,128)} %cls.1, f32[3,128,128]{2,1,0:T(8,128)} %coarse.1), custom_call_target="tpu_custom_call" | custom-call | tf_op jit(solution)/shard_map/fused/pallas_call | solution.py:1047
  60.9 1.3 %emit.1 = (f32[1,3,384,384]{3,2,1,0:T(8,128)}, f32[3,128,128]{2,1,0:T(8,128)}) custom-call(f32[1,3,384,384]{3,2,1,0:T(8,128)S(1)} %get-tuple-element.4.fine, f32[3,128,128]{2,1,0:T(8,128)S(1)} %get-tuple-element.5.coarse), custom_call_target="tpu_custom_call" | custom-call | tf_op jit(solution)/shard_map/emit/pallas_call | solution.py:1102
where the time goes:
time: 62.3 us; the launch traced here: 62.1 us
  Pallas kernels  61.5 us (99%)
  between operations  0.64 us (1%)
    pallas_call x1, Pallas kernels, fused(): pl.pallas_call(functools.partial(fused_kernel, nests, rows, cols), out_sh...  60.2 us
    pallas_call x1, Pallas kernels, emit(): pl.pallas_call(emit_kernel, out_shape=(jax.ShapeDtypeStruct(fine.shape, j...  1.28 us

commit v1 on v0

--- a/solution.py
+++ b/solution.py
@@ -12,7 +12,7 @@
 MESH = pl.DeviceIdType.MESH
 LANES = 128
 SUB = 8
-HEAD = 7
+HEAD = 3
 VMEM_BYTES = 67043328
 
 
@@ -548,9 +548,9 @@
 def fused_kernel(
     nests, rows, cols, anchor_in, levels_in, strips, wet, cls, coarse, fine, out,
     anchor, levels, fine_sem, held, wet_v, cls_v, coarse_v, pad, wet_p, bed_p, colh, rowh, cellh,
-    col_msg, row_msg, cell_msg, rest, above, spill, taken, load_sem,
+    col_msg, row_msg, cell_msg, rest, left, above, corner, weight, load_sem,
     big_send, big_recv, col_send, col_recv, row_send, row_recv, cell_send, cell_recv,
-    down_send, down_recv, side_send, side_recv,
+    side_send, side_recv, down_send, down_recv, far_send, far_recv, ready,
 ):
     parts = rows * cols
     nest, row, col = lax.axis_index("nest"), lax.axis_index("row"), lax.axis_index("col")
@@ -564,6 +564,7 @@
     end = SUB + tile_rows
     has_above, has_below = row > 0, row < rows - 1
     has_left, has_right = col > 0, col < cols - 1
+    has_last, has_next = block > 0, block < blocks - 1
 
     loads = [
         pltpu.make_async_copy(strips.at[0, :, :, 0], held, load_sem.at[0]),
@@ -584,26 +585,52 @@
     to_last = jnp.logical_and(row == 0, nest > 0)
     below_id = {"nest": (block + 1) // rows, "row": lax.rem(block + 1, rows), "col": col}
 
-    def greet(t, _):
+    def rank(q):
+        r = q // cols
+        return (r // 2 + lax.rem(r, 2) + lax.rem(q, cols)) * parts + q
+
+    mine = rank(me)
+
+    def greet(t, count):
         q = lax.rem(me + t, parts)
-        pl.semaphore_signal(barrier, inc=1, device_id=place(q), device_id_type=MESH)
+        later = rank(q) > mine
+
+        @pl.when(later)
+        def _():
+            pl.semaphore_signal(barrier, inc=1, device_id=place(q), device_id_type=MESH)
+
+        return count + jnp.where(later, 0, 1)
+
+    for at, takes in ((col, to_last), (col - 1, jnp.logical_and(to_last, has_left))):
+        @pl.when(takes)
+        def _(at=at):
+            pl.semaphore_signal(
+                barrier, inc=1, device_id={"nest": nest - 1, "row": rows - 1, "col": at},
+                device_id_type=MESH,
+            )
+
+    earlier = lax.fori_loop(1, parts, greet, 0) + jnp.where(to_next, 1, 0)
+    earlier = earlier + jnp.where(jnp.logical_and(to_next, has_right), 1, 0)
+
+    @pl.when(earlier > 0)
+    def _():
+        pl.semaphore_wait(barrier, earlier)
+
+    def answer(t, _):
+        q = lax.rem(me + t, parts)
+
+        @pl.when(rank(q) < mine)
+        def _():
+            pl.semaphore_signal(ready.at[me], inc=1, device_id=place(q), device_id_type=MESH)
+
         return 0
 
-    lax.fori_loop(1, parts, greet, 0)
-
-    @pl.when(to_next)
-    def _():
-        pl.semaphore_signal(barrier, inc=1, device_id=below_id, device_id_type=MESH)
-
-    @pl.when(to_last)
-    def _():
-        pl.semaphore_signal(
-            barrier, inc=1, device_id={"nest": nest - 1, "row": rows - 1, "col": col},
-            device_id_type=MESH,
-        )
-
-    peers = parts - 1 + jnp.where(to_next, 1, 0) + jnp.where(to_last, 1, 0)
-    pl.semaphore_wait(barrier, peers)
+    lax.fori_loop(1, parts, answer, 0)
+
+    def meet(q):
+        @pl.when(rank(q) > mine)
+        def _():
+            pl.semaphore_wait(ready.at[q], 1)
 
     def columns(c):
         return pl.ds(pl.multiple_of(c * tile_cols, LANES), tile_cols)
@@ -615,7 +642,7 @@
         return pltpu.make_async_remote_copy(
             src_ref=strips.at[0, :, q // cols, 0, :, columns(lax.rem(q, cols))],
             dst_ref=landing(me),
-            send_sem=big_send.at[q],
+            send_sem=big_send.at[0],
             recv_sem=big_recv.at[me],
             device_id=place(q),
             device_id_type=MESH,
@@ -625,8 +652,25 @@
         big(lax.rem(me + t, parts)).start()
         return 0
 
+    def stride(n):
+        if cols != 4:
+            return n
+        m = jnp.maximum(n - 2 * rows, 0)
+        near = jnp.where(col == 0, 1, 3) + cols * (n - 1)
+        far = jnp.where(col == 0, 2, 1) + lax.rem(m, 2) + cols * (m // 2)
+        t = jnp.where(n <= rows, near, jnp.where(n < 2 * rows, cols * (n - rows), far))
+        return jnp.where(jnp.logical_or(col == 1, col == 2), n, t)
+
+    def first_start(n, _):
+        t = stride(n)
+        meet(lax.rem(me + t, parts))
+        return big_start(t, 0)
+
+    def next_start(n, _):
+        return big_start(stride(n), 0)
+
     early = min(parts, HEAD)
-    lax.fori_loop(1, early, big_start, 0)
+    lax.fori_loop(1, early, first_start, 0)
     own = pltpu.make_async_copy(
         strips.at[0, :, row, 0, :, columns(col)], landing(me), big_recv.at[me]
     )
@@ -646,24 +690,23 @@
         for k in range(3):
             row_msg[0, j, k : k + 1, :] = held[k, j, band - 1 : band, :]
             row_msg[1, j, k : k + 1, :] = held[k, j, 0:1, :]
-    lane = iota((SUB, LANES), 1)
-    first = onehot(lane == 0)
-    last = onehot(lane == LANES - 1)
-    slot_of = iota((SUB, band), 0)
     col_msg[...] = jnp.zeros_like(col_msg)
+    lane = iota((3 * band, LANES), 1)
     for j in range(rows):
-        for c in range(cols):
-            message = jnp.zeros((SUB, band), jnp.float32)
-            for k in range(3):
-                if c > 0:
-                    for part in split(held[k, j, :, c * tile_cols - LANES : c * tile_cols], 3):
-                        message += jnp.where(slot_of == k, dot_t(last, part), 0.0)
-                if c < cols - 1:
-                    for part in split(
-                        held[k, j, :, (c + 1) * tile_cols : (c + 1) * tile_cols + LANES], 3
-                    ):
-                        message += jnp.where(slot_of == 3 + k, dot_t(first, part), 0.0)
-            col_msg[j * cols + c, :, 0:band] = message
+        for c in range(1, cols):
+            at = c * tile_cols
+            low = jnp.concatenate([held[k, j, :, at - LANES : at] for k in range(3)], axis=0)
+            high = jnp.concatenate([held[k, j, :, at : at + LANES] for k in range(3)], axis=0)
+            both = jnp.where(lane == 0, high, low).T
+            col_msg[j * cols + c, 0:1, 0 : 3 * band] = both[LANES - 1 : LANES]
+            col_msg[j * cols + c - 1, 1:2, 0 : 3 * band] = both[0:1]
+
+    def rest_meet(n, _):
+        meet(lax.rem(me + stride(n), parts))
+        return 0
+
+    if early < parts:
+        lax.fori_loop(early, parts, rest_meet, 0)
 
     cell_links = (
         (0, has_below, {"row": row + 1, "col": col}, has_above),
@@ -723,20 +766,20 @@
         return pltpu.make_async_remote_copy(
             src_ref=col_msg.at[q],
             dst_ref=colh.at[me],
-            send_sem=col_send.at[q],
+            send_sem=col_send.at[0],
             recv_sem=col_recv.at[me],
             device_id=place(q),
             device_id_type=MESH,
         )
 
-    def col_start(t, _):
-        col_copy(lax.rem(me + t, parts)).start()
+    def col_start(n, _):
+        col_copy(lax.rem(me + stride(n), parts)).start()
         return 0
 
     lax.fori_loop(1, parts, col_start, 0)
     pltpu.make_async_copy(col_msg.at[me], colh.at[me], col_recv.at[me]).start()
     if early < parts:
-        lax.fori_loop(early, parts, big_start, 0)
+        lax.fori_loop(early, parts, next_start, 0)
 
     loads[4].wait()
     loads[5].wait()
@@ -773,16 +816,15 @@
     for slot, _, target, receives in cell_links:
         @pl.when(jnp.logical_not(receives))
         def _(slot=slot):
-            cellh[slot] = jnp.zeros((SUB, LANES), jnp.int32)
+            cellh[slot] = jnp.zeros((2, LANES), jnp.int32)
 
         @pl.when(receives)
         def _(slot=slot, target=target):
             cell_copy(slot, target).wait_recv()
 
-    sub = iota((SUB, LANES), 0)
     for target, at, terms in ((wet_p, 0, 1), (bed_p, 1, 3)):
         def edge_of(slot, at=at):
-            cells = jnp.where(sub < 2, cellh[slot], 0)
+            cells = jnp.concatenate([cellh[slot], jnp.zeros((SUB - 2, LANES), jnp.int32)], axis=0)
             return cells.astype(jnp.float32) if at == 0 else look(cells)
 
         def row_of(slot, at=at, terms=terms):
@@ -801,16 +843,19 @@
         target[end : end + 1, 0:tile_cols] = jnp.where(has_below, row_of(1), 0.0)
         target[SUB:end, tile_cols:wide] = side(col_of(2), col_of(3))
 
-    for slot, receives, at in ((0, has_above, SUB - 1), (1, has_below, end)):
-        @pl.when(receives)
-        def _(slot=slot, at=at):
-            row_own(slot, 0, 0).wait()
-            for k in range(3):
-                pad[k, at : at + 1, 0:tile_cols] = rowh[slot, k : k + 1, :]
-
-    third = onehot(iota((group, band), 1) // 3 == iota((group, band), 0))
+    at_row = block * cell_rows + iota((cell_rows, cell_cols), 0)
+    at_col = col * cell_cols + iota((cell_rows, cell_cols), 1)
+    count = jnp.ones((cell_rows, cell_cols), jnp.float32)
+    for n in range(nests):
+        from_row = at_row - (n * rows * cell_rows + anchor[n, 0])
+        from_col = at_col - anchor[n, 1]
+        covered = (from_row >= 0) & (from_row < rows * cell_rows)
+        covered &= (from_col >= 0) & (from_col < cols * cell_cols)
+        count += jnp.where(covered, 1.0, 0.0)
+    weight[...] = 1.0 / count
+
+    third = onehot(iota((3 * group, 3 * band), 1) // 3 == iota((3 * group, 3 * band), 0))
     pick = onehot(iota((tile_cols, cell_cols), 0) // 3 == iota((tile_cols, cell_cols), 1))
-    unit = onehot(iota((band, LANES), 0) == iota((band, LANES), 1))
     window = band + 2 * SUB
 
     def west(x):
@@ -836,40 +881,122 @@
 
     def rest_rows(ref, b):
         return ref.at[:, pl.ds(pl.multiple_of(b * group, SUB), group), :]
+
+    def side_copy(b):
+        return pltpu.make_async_remote_copy(
+            src_ref=rest_rows(rest, b),
+            dst_ref=rest_rows(left, b),
+            send_sem=side_send.at[0],
+            recv_sem=side_recv.at[0],
+            device_id={"col": col + 1},
+            device_id_type=MESH,
+        )
 
     def down_copy(b):
         return pltpu.make_async_remote_copy(
             src_ref=rest_rows(rest, b),
             dst_ref=rest_rows(above, b),
-            send_sem=down_send.at[b],
-            recv_sem=down_recv.at[b],
+            send_sem=down_send.at[0],
+            recv_sem=down_recv.at[0],
             device_id=below_id,
             device_id_type=MESH,
         )
 
+    def far_copy(b):
+        return pltpu.make_async_remote_copy(
+            src_ref=rest_rows(rest, b),
+            dst_ref=rest_rows(corner, b),
+            send_sem=far_send.at[0],
+            recv_sem=far_recv.at[0],
+            device_id={**below_id, "col": col + 1},
+            device_id_type=MESH,
+        )
+
+    def share(s):
+        b = band_at(s)
+
+        @pl.when(has_right)
+        def _():
+            side_copy(b).start()
+
+        @pl.when(has_next)
+        def _():
+            down_copy(b).start()
+
+        @pl.when(jnp.logical_and(has_right, has_next))
+        def _():
+            far_copy(b).start()
+
+    last_three = parts - 2
+    if cols == 4:
+        last_three = jnp.where(col == 1, parts - 2, jnp.where(col == 2, parts - 4, parts - 3))
+
+    def turn(s, first):
+        t = jnp.where(s < first - 1, s + 1, s + 4)
+        return jnp.where(s < parts - 3, t, first + s - (parts - 3))
+
     def band_at(s):
-        return lax.rem(me - 1 - s + 2 * parts, parts)
+        return lax.rem(me + parts - turn(s, last_three), parts)
+
+    def restrict(b):
+        rows_of = pl.ds(pl.multiple_of(b * band, SUB), band)
+        value = jnp.concatenate([fine[0, k, rows_of, :] for k in range(3)], axis=0)
+        narrowed = dot(jnp.concatenate(split(value, 2), axis=0), pick)
+        mean = 0.0
+        for part in split(narrowed[: 3 * band] + narrowed[3 * band :], 2):
+            mean += dot(third, part)
+        mean = mean * (1.0 / 9.0)
+        cells = pl.ds(pl.multiple_of(b * group, SUB), group)
+        for k in range(3):
+            rest[k, cells, :] = mean[k * group : (k + 1) * group]
+
+    def arrived(t):
+        big_wait(lax.rem(me + parts - t, parts))
 
     def body(s, _):
         b = band_at(s)
+
+        @pl.when(s > 1)
+        def _():
+            share(s - 2)
 
         @pl.when(s == 0)
         def _():
             big_wait(me)
-            big_wait(band_at(0))
-
-        @pl.when(s < parts - 2)
+            arrived(1)
+
+        @pl.when(s < last_three - 1)
         def _():
-            big_wait(band_at(s + 1))
+            arrived(s + 2)
+
+        @pl.when(s == last_three - 1)
+        def _():
+            def others(t, _):
+                arrived(t)
+                return 0
+
+            lax.fori_loop(last_three + 2, parts, others, 0)
+
+        @pl.when(s == parts - 3)
+        def _():
+            arrived(last_three + 1)
 
         pltpu.make_async_copy(colh.at[b], colh.at[b], col_recv.at[b]).wait()
+        for slot, owner_band, receives, at in (
+            (0, 0, has_above, SUB - 1), (1, parts - 1, has_below, end)
+        ):
+            @pl.when(jnp.logical_and(b == owner_band, receives))
+            def _(slot=slot, at=at):
+                row_own(slot, 0, 0).wait()
+                for k in range(3):
+                    pad[k, at : at + 1, 0:tile_cols] = rowh[slot, k : k + 1, :]
+
         base = pl.multiple_of(b * band, SUB)
         inside = pl.ds(pl.multiple_of(base + SUB, SUB), band)
-        edges = 0.0
-        for part in split(colh[b], 3):
-            edges += dot_t(unit, part)
+        edges = jnp.concatenate([colh[b], jnp.zeros((SUB - 2, LANES), jnp.float32)], axis=0).T
         for k in range(3):
-            pad[k, inside, tile_cols:wide] = side(edges[:, k : k + 1], edges[:, 3 + k : 4 + k])
+            edge = edges[k * band : (k + 1) * band]
+            pad[k, inside, tile_cols:wide] = side(edge[:, 0:1], edge[:, 1:2])
 
         at = pl.ds(base, window)
         h, hu, hv = pad[0, at, :], pad[1, at, :], pad[2, at, :]
@@ -906,108 +1033,58 @@
             totals[k] += narrow(face - east(face))
         slope = gate * (bed_m - west(bed_m))
         totals[1] -= gravity * centre * narrow(slope + east(slope))
-        cells = pl.ds(pl.multiple_of(b * group, SUB), group)
         for k, state in enumerate((h_m, hu_m, hv_m)):
-            value = narrow(state) + totals[k]
-            fine[0, k, pl.ds(base, band), :] = value
-            summed = 0.0
-            for part in split(value, 2):
-                summed += dot(third, part)
-            mean = 0.0
-            for part in split(summed, 2):
-                mean += dot(part, pick)
-            rest[k, cells, :] = mean * (1.0 / 9.0)
-
-        @pl.when(jnp.logical_and(s > 0, block < blocks - 1))
-        def _():
-            down_copy(band_at(s - 1)).start()
-
+            fine[0, k, pl.ds(base, band), :] = narrow(state) + totals[k]
+        restrict(band_at(jnp.maximum(s - 1, 0)))
         return 0
 
     lax.fori_loop(0, parts, body, 0)
-
-    at_row = block * cell_rows + iota((cell_rows, cell_cols), 0)
-    at_col = col * cell_cols + iota((cell_rows, cell_cols), 1)
-    count = jnp.ones((cell_rows, cell_cols), jnp.float32)
-    for n in range(nests):
-        from_row = at_row - (n * rows * cell_rows + anchor[n, 0])
-        from_col = at_col - anchor[n, 1]
-        covered = (from_row >= 0) & (from_row < rows * cell_rows)
-        covered &= (from_col >= 0) & (from_col < cols * cell_cols)
-        count += jnp.where(covered, 1.0, 0.0)
-    weight = 1.0 / count
-
-    @pl.when(block < blocks - 1)
-    def _():
-        down_copy(me).start()
-
-    @pl.when(block == 0)
-    def _():
-        above[...] = jnp.zeros_like(above)
-
-    def down_wait(b, _):
-        down_copy(b).wait_recv()
-        return 0
-
-    @pl.when(block > 0)
-    def _():
-        lax.fori_loop(0, parts, down_wait, 0)
+    share(parts - 2)
+    restrict(band_at(parts - 1))
 
     source = jnp.maximum(block - 1, 0) // rows
-    r_at, r_from = iota((cell_rows, cell_rows), 0), iota((cell_rows, cell_rows), 1)
-    low_own = onehot(r_from + anchor[nest, 0] == r_at)
-    low_above = onehot(r_from + anchor[source, 0] == r_at + cell_rows)
-    c_from, c_at = iota((cell_cols, 2 * cell_cols), 0), iota((cell_cols, 2 * cell_cols), 1)
-    over_own = onehot(c_from + anchor[nest, 1] == c_at)
-    over_above = onehot(c_from + anchor[source, 1] == c_at)
-
-    def side_copy(k):
-        return pltpu.make_async_remote_copy(
-            src_ref=spill.at[k],
-            dst_ref=taken.at[k],
-            send_sem=side_send.at[k],
-            recv_sem=side_recv.at[k],
-            device_id={"col": col + 1},
-            device_id_type=MESH,
-        )
-
-    def side_start(k):
-        @pl.when(has_right)
-        def _():
-            side_copy(k).start()
+    row_own, col_own = anchor[nest, 0], anchor[nest, 1]
+    row_last, col_last = anchor[source, 0], anchor[source, 1]
+    cell_row = iota((cell_rows, cell_cols), 0)
+    cell_col = iota((cell_rows, cell_cols), 1)
+    share(parts - 1)
+
+    def settle(ref, sem):
+        pltpu.make_async_copy(ref, ref, sem.at[0]).wait()
+
+    def moved(cells, keep, by_col, from_row, by_row):
+        cells = jnp.where(keep, pltpu.roll(cells, by_col, 1), 0.0)
+        return jnp.where(from_row, pltpu.roll(cells, by_row, 0), 0.0)
 
     loads[3].wait()
     for k in range(3):
-        placed = 0.0
-        for cells, low, over in ((rest, low_own, over_own), (above, low_above, over_above)):
-            moved = 0.0
-            for part in split(cells[k], 2):
-                moved += dot(low, part)
-            for part in split(moved, 2):
-                placed += dot(part, over)
-        spill[k] = placed[:, cell_cols:]
-        if k > 0:
-            side_start(k - 1)
-        out[k] = coarse_v[k] + placed[:, :cell_cols]
-    side_start(2)
+        out[k] = coarse_v[k] + moved(
+            rest[k], cell_col >= col_own, col_own, cell_row >= row_own, row_own
+        )
+
+    @pl.when(has_left)
+    def _():
+        settle(left, side_recv)
+        for k in range(3):
+            out[k] += moved(left[k], cell_col < col_own, col_own, cell_row >= row_own, row_own)
+
+    @pl.when(has_last)
+    def _():
+        settle(above, down_recv)
+        for k in range(3):
+            out[k] += moved(above[k], cell_col >= col_last, col_last, cell_row < row_last, row_last)
+
+    @pl.when(jnp.logical_and(has_last, has_left))
+    def _():
+        settle(corner, far_recv)
+        for k in range(3):
+            out[k] += moved(corner[k], cell_col < col_last, col_last, cell_row < row_last, row_last)
+
     for k in range(3):
-        @pl.when(has_left)
-        def _(k=k):
-            side_copy(k).wait_recv()
-            out[k] = (out[k] + taken[k]) * weight
-
-        @pl.when(jnp.logical_not(has_left))
-        def _(k=k):
-            out[k] = out[k] * weight
-
-    def leave(t, _):
-        q = lax.rem(me + t, parts)
-        big(q).wait_send()
-        col_copy(q).wait_send()
-        return 0
-
-    lax.fori_loop(1, parts, leave, 0)
-
+        out[k] = out[k] * weight[...]
+
+    settle(pad.at[:, SUB : SUB + (parts - 1) * band, 0:tile_cols], big_send)
+    settle(colh.at[0 : parts - 1], col_send)
     for slot, sends, target, _ in cell_links:
         @pl.when(sends)
         def _(slot=slot, target=target):
@@ -1019,18 +1096,17 @@
                 if not mine:
                     row_copy(slot, j, c).wait_send()
 
-    def down_leave(b, _):
-        down_copy(b).wait_send()
-        return 0
-
-    @pl.when(block < blocks - 1)
-    def _():
-        lax.fori_loop(0, parts, down_leave, 0)
-
     @pl.when(has_right)
     def _():
-        for k in range(3):
-            side_copy(k).wait_send()
+        settle(rest, side_send)
+
+    @pl.when(has_next)
+    def _():
+        settle(rest, down_send)
+
+    @pl.when(jnp.logical_and(has_next, has_right))
+    def _():
+        settle(rest, far_send)
 
 
 def fused(nests, rows, cols, strips, anchor, wet, cls, levels, coarse):
@@ -1063,20 +1139,22 @@
             pltpu.VMEM((3,) + padded, f32),
             pltpu.VMEM(padded, f32),
             pltpu.VMEM(padded, f32),
-            pltpu.VMEM((parts, SUB, LANES), f32),
-            pltpu.VMEM((2, SUB, tile_cols), f32),
-            pltpu.VMEM((4, SUB, LANES), i32),
-            pltpu.VMEM((parts, SUB, LANES), f32),
-            pltpu.VMEM((2, blocks, SUB, full_cols), f32),
-            pltpu.VMEM((4, SUB, LANES), i32),
+            pltpu.VMEM((parts, 2, LANES), f32),
+            pltpu.VMEM((2, 4, tile_cols), f32),
+            pltpu.VMEM((4, 2, LANES), i32),
+            pltpu.VMEM((parts, 2, LANES), f32),
+            pltpu.VMEM((2, blocks, 4, full_cols), f32),
+            pltpu.VMEM((4, 2, LANES), i32),
             pltpu.VMEM(coarse.shape, f32),
             pltpu.VMEM(coarse.shape, f32),
             pltpu.VMEM(coarse.shape, f32),
             pltpu.VMEM(coarse.shape, f32),
+            pltpu.VMEM(cells, f32),
             dma((6,)),
-            dma((parts,)), dma((parts,)), dma((parts,)), dma((parts,)),
+            dma((1,)), dma((parts,)), dma((1,)), dma((parts,)),
             dma((2, rows, cols)), dma((2,)), dma((4,)), dma((4,)),
-            dma((parts,)), dma((parts,)), dma((3,)), dma((3,)),
+            dma((1,)), dma((1,)), dma((1,)), dma((1,)), dma((1,)), dma((1,)),
+            pltpu.SemaphoreType.REGULAR((parts,)),
         ],
         compiler_params=pltpu.CompilerParams(
             collective_id=2, has_side_effects=True, vmem_limit_bytes=VMEM_BYTES - results
@@ -1115,7 +1193,7 @@
 
 def local(nests, rows, cols, strips, anchor, wet_mask, bathy_index, bed_levels, coarse):
     band = strips.shape[4]
-    if band % (3 * SUB) == 0:
+    if band % (3 * SUB) == 0 and 3 * band <= LANES and rows * cols > 4:
         return emit(*fused(
             nests, rows, cols, strips, anchor, wet_mask, bathy_index, bed_levels, coarse
         ))

time: 62.3 us -> 55.2 us (0.89); the launches traced: 62.1 us -> 54.3 us
  Pallas kernels: 61.5 us -> 53.7 us
    pallas_call x1, Pallas kernels: 60.2 us -> 52.4 us  [fused(): pl.pallas_call(functools.partial(fused_kernel, nests, rows, cols), out_sh...]
where the time goes in v1:
time: 55.2 us; the launch traced here: 54.3 us
  Pallas kernels  53.7 us (97%)
  between operations  0.64 us (1%)
    pallas_call x1, Pallas kernels, fused(): pl.pallas_call(functools.partial(fused_kernel, nests, rows, cols), out_sh...  52.4 us
    pallas_call x1, Pallas kernels, emit(): pl.pallas_call(emit_kernel, out_shape=(jax.ShapeDtypeStruct(fine.shape, j...  1.28 us

profile of v1, /device:TPU:25, one launch (start us, length us, event | category | flops | bytes accessed | tf_op | source)
XLA Modules:
  0.0 54.3 jit_solution(16165185326151423635)
XLA Ops:
  0.6 52.4 %fused.1 = (f32[1,3,384,384]{3,2,1,0:T(8,128)S(1)}, f32[3,128,128]{2,1,0:T(8,128)S(1)}) custom-call(s32[2,2]{1,0:T(2,128)} %anchor_in.1, f32[16]{0:T(128)} %levels_in.1, f32[1,3,4,1,24,1536]{5,4,3,2,1,0:T(8,128)} %strips.1, s32[1,128,128]{2,1,0:T(8,128)} %wet.1, s32[1,128,128]{2,1,0:T(8,128)} %cls.1, f32[3,128,128]{2,1,0:T(8,128)} %coarse.1), custom_call_target="tpu_custom_call" | custom-call | tf_op jit(solution)/shard_map/fused/pallas_call | solution.py:1123
  53.0 1.3 %emit.1 = (f32[1,3,384,384]{3,2,1,0:T(8,128)}, f32[3,128,128]{2,1,0:T(8,128)}) custom-call(f32[1,3,384,384]{3,2,1,0:T(8,128)S(1)} %get-tuple-element.4.fine, f32[3,128,128]{2,1,0:T(8,128)S(1)} %get-tuple-element.5.coarse), custom_call_target="tpu_custom_call" | custom-call | tf_op jit(solution)/shard_map/emit/pallas_call | solution.py:1180

commit v2 on v1

--- a/solution.py
+++ b/solution.py
@@ -13,6 +13,7 @@
 LANES = 128
 SUB = 8
 HEAD = 3
+DIRECT = 9
 VMEM_BYTES = 67043328
 
 
@@ -550,7 +551,7 @@
     anchor, levels, fine_sem, held, wet_v, cls_v, coarse_v, pad, wet_p, bed_p, colh, rowh, cellh,
     col_msg, row_msg, cell_msg, rest, left, above, corner, weight, load_sem,
     big_send, big_recv, col_send, col_recv, row_send, row_recv, cell_send, cell_recv,
-    side_send, side_recv, down_send, down_recv, far_send, far_recv, ready,
+    side_send, side_recv, down_send, down_recv, far_send, far_recv, relay_send, ready,
 ):
     parts = rows * cols
     nest, row, col = lax.axis_index("nest"), lax.axis_index("row"), lax.axis_index("col")
@@ -591,6 +592,26 @@
 
     mine = rank(me)
 
+    def stride(n, col=col):
+        if cols != 4:
+            return n
+        m = jnp.maximum(n - 2 * rows, 0)
+        near = jnp.where(col == 0, 1, 3) + cols * (n - 1)
+        far = jnp.where(col == 0, 2, 1) + lax.rem(m, 2) + cols * (m // 2)
+        t = jnp.where(n <= rows, near, jnp.where(n < 2 * rows, cols * (n - rows), far))
+        first = jnp.where(lax.rem(n, cols) == 0, n + 1 - cols, n + 1)
+        first = jnp.where(n == parts - 1, parts + 1 - cols, first)
+        return jnp.where(col == 1, n, jnp.where(col == 2, first, t))
+
+    early = min(parts, HEAD)
+
+    def turn_of(source, q):
+        at = early - 1
+        for n in range(early - 1, 0, -1):
+            hit = lax.rem(source + stride(n, lax.rem(source, cols)), parts) == q
+            at = jnp.where(hit, n - 1, at)
+        return at
+
     def greet(t, count):
         q = lax.rem(me + t, parts)
         later = rank(q) > mine
@@ -621,16 +642,18 @@
 
         @pl.when(rank(q) < mine)
         def _():
-            pl.semaphore_signal(ready.at[me], inc=1, device_id=place(q), device_id_type=MESH)
+            pl.semaphore_signal(
+                ready.at[turn_of(q, me)], inc=1, device_id=place(q), device_id_type=MESH
+            )
 
         return 0
 
     lax.fori_loop(1, parts, answer, 0)
 
-    def meet(q):
-        @pl.when(rank(q) > mine)
+    def meet(n):
+        @pl.when(rank(lax.rem(me + stride(n), parts)) > mine)
         def _():
-            pl.semaphore_wait(ready.at[q], 1)
+            pl.semaphore_wait(ready.at[n - 1], 1)
 
     def columns(c):
         return pl.ds(pl.multiple_of(c * tile_cols, LANES), tile_cols)
@@ -652,24 +675,13 @@
         big(lax.rem(me + t, parts)).start()
         return 0
 
-    def stride(n):
-        if cols != 4:
-            return n
-        m = jnp.maximum(n - 2 * rows, 0)
-        near = jnp.where(col == 0, 1, 3) + cols * (n - 1)
-        far = jnp.where(col == 0, 2, 1) + lax.rem(m, 2) + cols * (m // 2)
-        t = jnp.where(n <= rows, near, jnp.where(n < 2 * rows, cols * (n - rows), far))
-        return jnp.where(jnp.logical_or(col == 1, col == 2), n, t)
-
     def first_start(n, _):
-        t = stride(n)
-        meet(lax.rem(me + t, parts))
-        return big_start(t, 0)
+        meet(n)
+        return big_start(stride(n), 0)
 
     def next_start(n, _):
         return big_start(stride(n), 0)
 
-    early = min(parts, HEAD)
     lax.fori_loop(1, early, first_start, 0)
     own = pltpu.make_async_copy(
         strips.at[0, :, row, 0, :, columns(col)], landing(me), big_recv.at[me]
@@ -701,12 +713,14 @@
             col_msg[j * cols + c, 0:1, 0 : 3 * band] = both[LANES - 1 : LANES]
             col_msg[j * cols + c - 1, 1:2, 0 : 3 * band] = both[0:1]
 
-    def rest_meet(n, _):
-        meet(lax.rem(me + stride(n), parts))
-        return 0
-
-    if early < parts:
-        lax.fori_loop(early, parts, rest_meet, 0)
+    def later(n, count):
+        return count + jnp.where(rank(lax.rem(me + stride(n), parts)) > mine, 1, 0)
+
+    rest_of = lax.fori_loop(early, parts, later, 0)
+
+    @pl.when(rest_of > 0)
+    def _():
+        pl.semaphore_wait(ready.at[early - 1], rest_of)
 
     cell_links = (
         (0, has_below, {"row": row + 1, "col": col}, has_above),
@@ -734,7 +748,7 @@
         return pltpu.make_async_remote_copy(
             src_ref=row_msg.at[slot, j, :, c * tile_cols : (c + 1) * tile_cols],
             dst_ref=rowh.at[slot],
-            send_sem=row_send.at[slot, j, c],
+            send_sem=row_send.at[j],
             recv_sem=row_recv.at[slot],
             device_id={"row": j + 1 if slot == 0 else j - 1, "col": c},
             device_id_type=MESH,
@@ -767,7 +781,7 @@
             src_ref=col_msg.at[q],
             dst_ref=colh.at[me],
             send_sem=col_send.at[0],
-            recv_sem=col_recv.at[me],
+            recv_sem=col_recv.at[0],
             device_id=place(q),
             device_id_type=MESH,
         )
@@ -777,7 +791,7 @@
         return 0
 
     lax.fori_loop(1, parts, col_start, 0)
-    pltpu.make_async_copy(col_msg.at[me], colh.at[me], col_recv.at[me]).start()
+    pltpu.make_async_copy(col_msg.at[me], colh.at[me], col_recv.at[0]).start()
     if early < parts:
         lax.fori_loop(early, parts, next_start, 0)
 
@@ -811,7 +825,6 @@
     for k in range(3):
         pad[k, 0:SUB, :] = zeros
         pad[k, end : end + SUB, :] = zeros
-        pad[k, SUB:end, tile_cols:wide] = jnp.zeros((tile_rows, LANES), jnp.float32)
 
     for slot, _, target, receives in cell_links:
         @pl.when(jnp.logical_not(receives))
@@ -842,6 +855,19 @@
         target[SUB - 1 : SUB, 0:tile_cols] = jnp.where(has_above, row_of(0), 0.0)
         target[end : end + 1, 0:tile_cols] = jnp.where(has_below, row_of(1), 0.0)
         target[SUB:end, tile_cols:wide] = side(col_of(2), col_of(3))
+
+    def settle(ref, sem):
+        pltpu.make_async_copy(ref, ref, sem.at[0]).wait()
+
+    settle(colh, col_recv)
+    edges = jnp.concatenate([colh[b] for b in range(parts)], axis=0).T
+    for k in range(3):
+        edge = edges[k * band : (k + 1) * band]
+        for b in range(parts):
+            top = SUB + b * band
+            pad[k, top : top + band, tile_cols:wide] = side(
+                edge[:, 2 * b : 2 * b + 1], edge[:, 2 * b + 1 : 2 * b + 2]
+            )
 
     at_row = block * cell_rows + iota((cell_rows, cell_cols), 0)
     at_col = col * cell_cols + iota((cell_rows, cell_cols), 1)
@@ -854,9 +880,7 @@
         count += jnp.where(covered, 1.0, 0.0)
     weight[...] = 1.0 / count
 
-    third = onehot(iota((3 * group, 3 * band), 1) // 3 == iota((3 * group, 3 * band), 0))
     pick = onehot(iota((tile_cols, cell_cols), 0) // 3 == iota((tile_cols, cell_cols), 1))
-    window = band + 2 * SUB
 
     def west(x):
         return pltpu.roll(x, 1, 1)
@@ -870,9 +894,6 @@
     def south(x):
         return pltpu.roll(x, x.shape[0] - 1, 0)
 
-    def mid(x):
-        return x[SUB : SUB + band]
-
     def narrow(x):
         return x[:, 0:tile_cols]
 
@@ -882,12 +903,14 @@
     def rest_rows(ref, b):
         return ref.at[:, pl.ds(pl.multiple_of(b * group, SUB), group), :]
 
-    def side_copy(b):
+    middle = cols // 2
+
+    def side_copy(b, slot):
         return pltpu.make_async_remote_copy(
             src_ref=rest_rows(rest, b),
             dst_ref=rest_rows(left, b),
             send_sem=side_send.at[0],
-            recv_sem=side_recv.at[0],
+            recv_sem=side_recv.at[slot],
             device_id={"col": col + 1},
             device_id_type=MESH,
         )
@@ -912,20 +935,45 @@
             device_id_type=MESH,
         )
 
+    def relay_copy(b):
+        return pltpu.make_async_remote_copy(
+            src_ref=rest_rows(left, b),
+            dst_ref=rest_rows(corner, b),
+            send_sem=relay_send.at[0],
+            recv_sem=far_recv.at[0],
+            device_id=below_id,
+            device_id_type=MESH,
+        )
+
     def share(s):
         b = band_at(s)
 
-        @pl.when(has_right)
+        @pl.when(jnp.logical_and(has_right, col + 1 != middle))
         def _():
-            side_copy(b).start()
+            side_copy(b, parts).start()
 
         @pl.when(has_next)
         def _():
             down_copy(b).start()
 
-        @pl.when(jnp.logical_and(has_right, has_next))
+        @pl.when(jnp.logical_and(jnp.logical_and(has_right, has_next), col + 1 != middle))
         def _():
             far_copy(b).start()
+
+    def share_middle(first, last):
+        def one(s, _):
+            b = band_at(s)
+            side_copy(b, jnp.where(s < parts - DIRECT, b, parts)).start()
+
+            @pl.when(jnp.logical_and(has_next, s >= parts - DIRECT))
+            def _():
+                far_copy(b).start()
+
+            return 0
+
+        @pl.when(col + 1 == middle)
+        def _():
+            lax.fori_loop(first, last, one, 0)
 
     last_three = parts - 2
     if cols == 4:
@@ -938,67 +986,12 @@
     def band_at(s):
         return lax.rem(me + parts - turn(s, last_three), parts)
 
-    def restrict(b):
-        rows_of = pl.ds(pl.multiple_of(b * band, SUB), band)
-        value = jnp.concatenate([fine[0, k, rows_of, :] for k in range(3)], axis=0)
-        narrowed = dot(jnp.concatenate(split(value, 2), axis=0), pick)
-        mean = 0.0
-        for part in split(narrowed[: 3 * band] + narrowed[3 * band :], 2):
-            mean += dot(third, part)
-        mean = mean * (1.0 / 9.0)
-        cells = pl.ds(pl.multiple_of(b * group, SUB), group)
-        for k in range(3):
-            rest[k, cells, :] = mean[k * group : (k + 1) * group]
-
-    def arrived(t):
-        big_wait(lax.rem(me + parts - t, parts))
-
-    def body(s, _):
-        b = band_at(s)
-
-        @pl.when(s > 1)
-        def _():
-            share(s - 2)
-
-        @pl.when(s == 0)
-        def _():
-            big_wait(me)
-            arrived(1)
-
-        @pl.when(s < last_three - 1)
-        def _():
-            arrived(s + 2)
-
-        @pl.when(s == last_three - 1)
-        def _():
-            def others(t, _):
-                arrived(t)
-                return 0
-
-            lax.fori_loop(last_three + 2, parts, others, 0)
-
-        @pl.when(s == parts - 3)
-        def _():
-            arrived(last_three + 1)
-
-        pltpu.make_async_copy(colh.at[b], colh.at[b], col_recv.at[b]).wait()
-        for slot, owner_band, receives, at in (
-            (0, 0, has_above, SUB - 1), (1, parts - 1, has_below, end)
-        ):
-            @pl.when(jnp.logical_and(b == owner_band, receives))
-            def _(slot=slot, at=at):
-                row_own(slot, 0, 0).wait()
-                for k in range(3):
-                    pad[k, at : at + 1, 0:tile_cols] = rowh[slot, k : k + 1, :]
-
-        base = pl.multiple_of(b * band, SUB)
-        inside = pl.ds(pl.multiple_of(base + SUB, SUB), band)
-        edges = jnp.concatenate([colh[b], jnp.zeros((SUB - 2, LANES), jnp.float32)], axis=0).T
-        for k in range(3):
-            edge = edges[k * band : (k + 1) * band]
-            pad[k, inside, tile_cols:wide] = side(edge[:, 0:1], edge[:, 1:2])
-
-        at = pl.ds(base, window)
+    def advance(base, count):
+        def mid(x):
+            return x[SUB : SUB + count]
+
+        base = pl.multiple_of(base, SUB)
+        at = pl.ds(base, count + 2 * SUB)
         h, hu, hv = pad[0, at, :], pad[1, at, :], pad[2, at, :]
         wet_w, bed_w = wet_p[at, :], bed_p[at, :]
         safe = jnp.where(wet_w > 0.5, h, 1.0)
@@ -1034,24 +1027,83 @@
         slope = gate * (bed_m - west(bed_m))
         totals[1] -= gravity * centre * narrow(slope + east(slope))
         for k, state in enumerate((h_m, hu_m, hv_m)):
-            fine[0, k, pl.ds(base, band), :] = narrow(state) + totals[k]
-        restrict(band_at(jnp.maximum(s - 1, 0)))
+            fine[0, k, pl.ds(base, count), :] = narrow(state) + totals[k]
+
+    def restrict(base, count):
+        rows_of = pl.ds(pl.multiple_of(base, SUB), count)
+        value = jnp.concatenate([fine[0, k, rows_of, :] for k in range(3)], axis=0)
+        narrowed = dot(jnp.concatenate(split(value, 2), axis=0), pick)
+        third = onehot(iota((count, 3 * count), 1) // 3 == iota((count, 3 * count), 0))
+        mean = 0.0
+        for part in split(narrowed[: 3 * count] + narrowed[3 * count :], 2):
+            mean += dot(third, part)
+        mean = mean * (1.0 / 9.0)
+        cells = pl.ds(pl.multiple_of(base // 3, SUB), count // 3)
+        for k in range(3):
+            rest[k, cells, :] = mean[k * count // 3 : (k + 1) * count // 3]
+
+    def arrived(t):
+        big_wait(lax.rem(me + parts - t, parts))
+
+    def halo(lowest, highest):
+        for slot, edge, receives, at in ((0, 0, has_above, SUB - 1), (1, parts - 1, has_below, end)):
+            here = jnp.logical_and(lowest <= edge, edge <= highest)
+
+            @pl.when(jnp.logical_and(here, receives))
+            def _(slot=slot, at=at):
+                row_own(slot, 0, 0).wait()
+                for k in range(3):
+                    pad[k, at : at + 1, 0:tile_cols] = rowh[slot, k : k + 1, :]
+
+    def body(s, _):
+        b = band_at(s)
+
+        @pl.when(s > 1)
+        def _():
+            share(s - 2)
+
+        @pl.when(s == 0)
+        def _():
+            big_wait(me)
+            arrived(1)
+
+        @pl.when(s < last_three - 1)
+        def _():
+            arrived(s + 2)
+
+        @pl.when(s == last_three - 1)
+        def _():
+            def others(t, _):
+                arrived(t)
+                return 0
+
+            lax.fori_loop(last_three + 2, parts, others, 0)
+
+        halo(b, b)
+        advance(b * band, band)
+        restrict(band_at(jnp.maximum(s - 1, 0)) * band, band)
         return 0
 
-    lax.fori_loop(0, parts, body, 0)
-    share(parts - 2)
-    restrict(band_at(parts - 1))
+    lax.fori_loop(0, parts - 3, body, 0)
+    share(parts - 5)
+    share_middle(0, parts - 4)
+    restrict(band_at(parts - 4) * band, band)
+    arrived(last_three + 1)
+    share(parts - 4)
+    share_middle(parts - 4, parts - 3)
+    lowest = band_at(parts - 1)
+    halo(lowest, lowest + 2)
+    advance(lowest * band, 3 * band)
+    restrict(lowest * band, 3 * band)
+    for s in range(parts - 3, parts):
+        share(s)
+    share_middle(parts - 3, parts)
 
     source = jnp.maximum(block - 1, 0) // rows
     row_own, col_own = anchor[nest, 0], anchor[nest, 1]
     row_last, col_last = anchor[source, 0], anchor[source, 1]
     cell_row = iota((cell_rows, cell_cols), 0)
     cell_col = iota((cell_rows, cell_cols), 1)
-    share(parts - 1)
-
-    def settle(ref, sem):
-        pltpu.make_async_copy(ref, ref, sem.at[0]).wait()
-
     def moved(cells, keep, by_col, from_row, by_row):
         cells = jnp.where(keep, pltpu.roll(cells, by_col, 1), 0.0)
         return jnp.where(from_row, pltpu.roll(cells, by_row, 0), 0.0)
@@ -1062,9 +1114,31 @@
             rest[k], cell_col >= col_own, col_own, cell_row >= row_own, row_own
         )
 
+    left_three = parts - 2 if cols == 4 else last_three
+
+    def relay(t, _):
+        b = lax.rem(me + 2 * parts - 1 - turn(t, left_three), parts)
+        pltpu.make_async_copy(rest_rows(left, b), rest_rows(left, b), side_recv.at[b]).wait()
+
+        @pl.when(has_next)
+        def _():
+            relay_copy(b).start()
+
+        return 0
+
+    few = DIRECT * group
+
+    @pl.when(jnp.logical_and(has_left, col == middle))
+    def _():
+        lax.fori_loop(0, parts - DIRECT, relay, 0)
+        pltpu.make_async_copy(rest.at[:, :few], left.at[:, :few], side_recv.at[parts]).wait()
+
+    @pl.when(jnp.logical_and(has_left, col != middle))
+    def _():
+        pltpu.make_async_copy(rest, left, side_recv.at[parts]).wait()
+
     @pl.when(has_left)
     def _():
-        settle(left, side_recv)
         for k in range(3):
             out[k] += moved(left[k], cell_col < col_own, col_own, cell_row >= row_own, row_own)
 
@@ -1092,9 +1166,11 @@
     for slot in range(2):
         @pl.when(me == owner[slot])
         def _(slot=slot):
-            for j, c, mine in row_targets(slot):
-                if not mine:
-                    row_copy(slot, j, c).wait_send()
+            for row_at in range(rows):
+                n = sum(j == row_at and not mine for j, _, mine in row_targets(slot))
+                if n > 0:
+                    sent = row_msg.at[slot, row_at, :, 0 : n * tile_cols]
+                    pltpu.make_async_copy(sent, sent, row_send.at[row_at]).wait()
 
     @pl.when(has_right)
     def _():
@@ -1104,9 +1180,17 @@
     def _():
         settle(rest, down_send)
 
-    @pl.when(jnp.logical_and(has_next, has_right))
+    @pl.when(jnp.logical_and(jnp.logical_and(has_next, has_right), col + 1 != middle))
     def _():
         settle(rest, far_send)
+
+    @pl.when(jnp.logical_and(jnp.logical_and(has_next, has_right), col + 1 == middle))
+    def _():
+        settle(rest.at[:, :few], far_send)
+
+    @pl.when(jnp.logical_and(jnp.logical_and(has_next, has_left), col == middle))
+    def _():
+        settle(rest.at[:, few:], relay_send)
 
 
 def fused(nests, rows, cols, strips, anchor, wet, cls, levels, coarse):
@@ -1151,10 +1235,10 @@
             pltpu.VMEM(coarse.shape, f32),
             pltpu.VMEM(cells, f32),
             dma((6,)),
-            dma((1,)), dma((parts,)), dma((1,)), dma((parts,)),
-            dma((2, rows, cols)), dma((2,)), dma((4,)), dma((4,)),
-            dma((1,)), dma((1,)), dma((1,)), dma((1,)), dma((1,)), dma((1,)),
-            pltpu.SemaphoreType.REGULAR((parts,)),
+            dma((1,)), dma((parts,)), dma((1,)), dma((1,)),
+            dma((rows,)), dma((2,)), dma((4,)), dma((4,)),
+            dma((1,)), dma((parts + 1,)), dma((1,)), dma((1,)), dma((1,)), dma((1,)), dma((1,)),
+            pltpu.SemaphoreType.REGULAR((HEAD,)),
         ],
         compiler_params=pltpu.CompilerParams(
             collective_id=2, has_side_effects=True, vmem_limit_bytes=VMEM_BYTES - results
@@ -1193,7 +1277,7 @@
 
 def local(nests, rows, cols, strips, anchor, wet_mask, bathy_index, bed_levels, coarse):
     band = strips.shape[4]
-    if band % (3 * SUB) == 0 and 3 * band <= LANES and rows * cols > 4:
+    if band % (3 * SUB) == 0 and 3 * band <= LANES and rows > 1 and cols == 4:
         return emit(*fused(
             nests, rows, cols, strips, anchor, wet_mask, bathy_index, bed_levels, coarse
         ))

time: 55.2 us -> 53 us (0.960); the launches traced: 54.3 us -> 52.7 us
  Pallas kernels: 53.7 us -> 52 us
    pallas_call x1, Pallas kernels: 52.4 us -> 50.8 us  [fused(): pl.pallas_call(functools.partial(fused_kernel, nests, rows, cols), out_sh...]
where the time goes in v2:
time: 53 us; the launch traced here: 52.7 us
  Pallas kernels  52 us (98%)
  between operations  0.64 us (1%)
    pallas_call x1, Pallas kernels, fused(): pl.pallas_call(functools.partial(fused_kernel, nests, rows, cols), out_sh...  50.8 us
    pallas_call x1, Pallas kernels, emit(): pl.pallas_call(emit_kernel, out_shape=(jax.ShapeDtypeStruct(fine.shape, j...  1.28 us

profile of v2, /device:TPU:25, one launch (start us, length us, event | category | flops | bytes accessed | tf_op | source)
XLA Modules:
  0.0 52.7 jit_solution(777058263623272469)
XLA Ops:
  0.6 50.8 %fused.1 = (f32[1,3,384,384]{3,2,1,0:T(8,128)S(1)}, f32[3,128,128]{2,1,0:T(8,128)S(1)}) custom-call(s32[2,2]{1,0:T(2,128)} %anchor_in.1, f32[16]{0:T(128)} %levels_in.1, f32[1,3,4,1,24,1536]{5,4,3,2,1,0:T(8,128)} %strips.1, s32[1,128,128]{2,1,0:T(8,128)} %wet.1, s32[1,128,128]{2,1,0:T(8,128)} %cls.1, f32[3,128,128]{2,1,0:T(8,128)} %coarse.1), custom_call_target="tpu_custom_call" | custom-call | tf_op jit(solution)/shard_map/fused/pallas_call | solution.py:1207
  51.4 1.3 %emit.1 = (f32[1,3,384,384]{3,2,1,0:T(8,128)}, f32[3,128,128]{2,1,0:T(8,128)}) custom-call(f32[1,3,384,384]{3,2,1,0:T(8,128)S(1)} %get-tuple-element.4.fine, f32[3,128,128]{2,1,0:T(8,128)S(1)} %get-tuple-element.5.coarse), custom_call_target="tpu_custom_call" | custom-call | tf_op jit(solution)/shard_map/emit/pallas_call | solution.py:1264

commit v3 on v2

--- a/solution.py
+++ b/solution.py
@@ -588,7 +588,8 @@
 
     def rank(q):
         r = q // cols
-        return (r // 2 + lax.rem(r, 2) + lax.rem(q, cols)) * parts + q
+        c = lax.rem(q, cols)
+        return (2 * (r // 2 + lax.rem(r, 2) + c) + jnp.where(c == 2, 0, 1)) * parts + q
 
     mine = rank(me)
 
@@ -950,7 +951,7 @@
 
         @pl.when(jnp.logical_and(has_right, col + 1 != middle))
         def _():
-            side_copy(b, parts).start()
+            side_copy(b, parts - DIRECT).start()
 
         @pl.when(has_next)
         def _():
@@ -963,7 +964,7 @@
     def share_middle(first, last):
         def one(s, _):
             b = band_at(s)
-            side_copy(b, jnp.where(s < parts - DIRECT, b, parts)).start()
+            side_copy(b, jnp.minimum(s, parts - DIRECT)).start()
 
             @pl.when(jnp.logical_and(has_next, s >= parts - DIRECT))
             def _():
@@ -1118,7 +1119,7 @@
 
     def relay(t, _):
         b = lax.rem(me + 2 * parts - 1 - turn(t, left_three), parts)
-        pltpu.make_async_copy(rest_rows(left, b), rest_rows(left, b), side_recv.at[b]).wait()
+        pltpu.make_async_copy(rest_rows(left, b), rest_rows(left, b), side_recv.at[t]).wait()
 
         @pl.when(has_next)
         def _():
@@ -1131,11 +1132,11 @@
     @pl.when(jnp.logical_and(has_left, col == middle))
     def _():
         lax.fori_loop(0, parts - DIRECT, relay, 0)
-        pltpu.make_async_copy(rest.at[:, :few], left.at[:, :few], side_recv.at[parts]).wait()
+        pltpu.make_async_copy(rest.at[:, :few], left.at[:, :few], side_recv.at[parts - DIRECT]).wait()
 
     @pl.when(jnp.logical_and(has_left, col != middle))
     def _():
-        pltpu.make_async_copy(rest, left, side_recv.at[parts]).wait()
+        pltpu.make_async_copy(rest, left, side_recv.at[parts - DIRECT]).wait()
 
     @pl.when(has_left)
     def _():
@@ -1237,7 +1238,7 @@
             dma((6,)),
             dma((1,)), dma((parts,)), dma((1,)), dma((1,)),
             dma((rows,)), dma((2,)), dma((4,)), dma((4,)),
-            dma((1,)), dma((parts + 1,)), dma((1,)), dma((1,)), dma((1,)), dma((1,)), dma((1,)),
+            dma((1,)), dma((parts - DIRECT + 1,)), dma((1,)), dma((1,)), dma((1,)), dma((1,)), dma((1,)),
             pltpu.SemaphoreType.REGULAR((HEAD,)),
         ],
         compiler_params=pltpu.CompilerParams(
@@ -1277,7 +1278,7 @@
 
 def local(nests, rows, cols, strips, anchor, wet_mask, bathy_index, bed_levels, coarse):
     band = strips.shape[4]
-    if band % (3 * SUB) == 0 and 3 * band <= LANES and rows > 1 and cols == 4:
+    if band % (3 * SUB) == 0 and 3 * band <= LANES and rows * cols > DIRECT + 3 and cols == 4:
         return emit(*fused(
             nests, rows, cols, strips, anchor, wet_mask, bathy_index, bed_levels, coarse
         ))

time: 53 us -> 52.9 us (level)
  no operation moved by 1% of the time
where the time goes in v3:
time: 52.9 us; the launch traced here: 52.6 us
  Pallas kernels  52 us (98%)
  between operations  0.64 us (1%)
    pallas_call x1, Pallas kernels, fused(): pl.pallas_call(functools.partial(fused_kernel, nests, rows, cols), out_sh...  50.7 us
    pallas_call x1, Pallas kernels, emit(): pl.pallas_call(emit_kernel, out_shape=(jax.ShapeDtypeStruct(fine.shape, j...  1.28 us

profile of v3, /device:TPU:25, one launch (start us, length us, event | category | flops | bytes accessed | tf_op | source)
XLA Modules:
  0.0 52.6 jit_solution(7564238748991215881)
XLA Ops:
  0.6 50.7 %fused.1 = (f32[1,3,384,384]{3,2,1,0:T(8,128)S(1)}, f32[3,128,128]{2,1,0:T(8,128)S(1)}) custom-call(s32[2,2]{1,0:T(2,128)} %anchor_in.1, f32[16]{0:T(128)} %levels_in.1, f32[1,3,4,1,24,1536]{5,4,3,2,1,0:T(8,128)} %strips.1, s32[1,128,128]{2,1,0:T(8,128)} %wet.1, s32[1,128,128]{2,1,0:T(8,128)} %cls.1, f32[3,128,128]{2,1,0:T(8,128)} %coarse.1), custom_call_target="tpu_custom_call" | custom-call | tf_op jit(solution)/shard_map/fused/pallas_call | solution.py:1208
  51.3 1.3 %emit.1 = (f32[1,3,384,384]{3,2,1,0:T(8,128)}, f32[3,128,128]{2,1,0:T(8,128)}) custom-call(f32[1,3,384,384]{3,2,1,0:T(8,128)S(1)} %get-tuple-element.4.fine, f32[3,128,128]{2,1,0:T(8,128)S(1)} %get-tuple-element.5.coarse), custom_call_target="tpu_custom_call" | custom-call | tf_op jit(solution)/shard_map/emit/pallas_call | solution.py:1265

commit v4 on v3

--- a/solution.py
+++ b/solution.py
@@ -1089,12 +1089,14 @@
     share(parts - 5)
     share_middle(0, parts - 4)
     restrict(band_at(parts - 4) * band, band)
+    lowest = band_at(parts - 1)
+    halo(lowest, lowest + 2)
+    advance(lowest * band, band - SUB)
+    advance((lowest + 2) * band + SUB, band - SUB)
     arrived(last_three + 1)
     share(parts - 4)
     share_middle(parts - 4, parts - 3)
-    lowest = band_at(parts - 1)
-    halo(lowest, lowest + 2)
-    advance(lowest * band, 3 * band)
+    advance((lowest + 1) * band - SUB, band + 2 * SUB)
     restrict(lowest * band, 3 * band)
     for s in range(parts - 3, parts):
         share(s)

time: 52.9 us -> 52.9 us (level)
  no operation moved by 1% of the time
where the time goes in v4:
time: 52.9 us; the launch traced here: 52.5 us
  Pallas kernels  51.8 us (98%)
  between operations  0.64 us (1%)
    pallas_call x1, Pallas kernels, fused(): pl.pallas_call(functools.partial(fused_kernel, nests, rows, cols), out_sh...  50.6 us
    pallas_call x1, Pallas kernels, emit(): pl.pallas_call(emit_kernel, out_shape=(jax.ShapeDtypeStruct(fine.shape, j...  1.28 us

profile of v4, /device:TPU:25, one launch (start us, length us, event | category | flops | bytes accessed | tf_op | source)
XLA Modules:
  0.0 52.5 jit_solution(10262228236734129913)
XLA Ops:
  0.6 50.6 %fused.1 = (f32[1,3,384,384]{3,2,1,0:T(8,128)S(1)}, f32[3,128,128]{2,1,0:T(8,128)S(1)}) custom-call(s32[2,2]{1,0:T(2,128)} %anchor_in.1, f32[16]{0:T(128)} %levels_in.1, f32[1,3,4,1,24,1536]{5,4,3,2,1,0:T(8,128)} %strips.1, s32[1,128,128]{2,1,0:T(8,128)} %wet.1, s32[1,128,128]{2,1,0:T(8,128)} %cls.1, f32[3,128,128]{2,1,0:T(8,128)} %coarse.1), custom_call_target="tpu_custom_call" | custom-call | tf_op jit(solution)/shard_map/fused/pallas_call | solution.py:1210
  51.2 1.3 %emit.1 = (f32[1,3,384,384]{3,2,1,0:T(8,128)}, f32[3,128,128]{2,1,0:T(8,128)}) custom-call(f32[1,3,384,384]{3,2,1,0:T(8,128)S(1)} %get-tuple-element.4.fine, f32[3,128,128]{2,1,0:T(8,128)S(1)} %get-tuple-element.5.coarse), custom_call_target="tpu_custom_call" | custom-call | tf_op jit(solution)/shard_map/emit/pallas_call | solution.py:1267
